TPU v7x, 32 devices: a whole 2x2x4 slice. The times are simulated.
32 devices in a mesh: stage: 4 (over z), data: 8 (over y, x, core).
Axes of the slice: x: 2, y: 2, z: 4, core: 2. Of those that a mesh axis runs over, the one named last changes fastest.
Arguments:
- tokens_in: bfloat16 [32, 64, 1280], P('data')
- targets: bfloat16 [32, 64, 1280], P('data')
- w_up: bfloat16 [2, 4, 1280, 5120], P(None, 'stage')
- w_down: bfloat16 [2, 4, 5120, 1280], P(None, 'stage')
Outputs:
- output 1: float32 [], replicated
- output 2: float32 [2, 4, 1280, 5120], P(None, 'stage', 'data')
- output 3: float32 [2, 4, 5120, 1280], P(None, 'stage', 'data')
All inputs are finite; a program needn't handle non-finite values.
Results may differ from a plain program's by a relative error of at most 0.00283349.
Values are sent between devices in bfloat16 or wider.
A program may use at most 1 GiB of HBM per device.

v0:
```python
import jax
import jax.numpy as jnp
from jax import lax
from jax.sharding import PartitionSpec as P


def gelu_fn(pre_act):
    return jax.nn.gelu(pre_act, approximate=True)


def layer_fwd(h_in, w_one, w_two):
    pre_act = jnp.dot(h_in, w_one, preferred_element_type=jnp.float32)
    act_bf = gelu_fn(pre_act).astype(jnp.bfloat16)
    out_val = h_in.astype(jnp.float32) + jnp.dot(act_bf, w_two, preferred_element_type=jnp.float32)
    return out_val.astype(jnp.bfloat16)


def layer_bwd(h_in, grad_out, w_one, w_two):
    pre_act = jnp.dot(h_in, w_one, preferred_element_type=jnp.float32)
    act_val, gelu_vjp = jax.vjp(gelu_fn, pre_act)
    act_bf = act_val.astype(jnp.bfloat16)
    g_down = jnp.einsum("tf,td->fd", act_bf, grad_out, preferred_element_type=jnp.float32)
    d_act = jnp.einsum("td,fd->tf", grad_out, w_two, preferred_element_type=jnp.float32).astype(jnp.bfloat16)
    d_pre = gelu_vjp(d_act.astype(jnp.float32))[0].astype(jnp.bfloat16)
    g_up = jnp.einsum("td,tf->df", h_in, d_pre, preferred_element_type=jnp.float32)
    back_val = jnp.einsum("tf,df->td", d_pre, w_one, preferred_element_type=jnp.float32)
    d_in = (grad_out.astype(jnp.float32) + back_val).astype(jnp.bfloat16)
    return d_in, g_up, g_down


def add_layer(acc_arr, new_part, layer_idx):
    start_idx = (layer_idx, 0, 0)
    old_val = lax.dynamic_slice(acc_arr, start_idx, (1,) + new_part.shape)
    return lax.dynamic_update_slice(acc_arr, old_val + new_part[None], start_idx)


def make_tick(n_stage, n_micro, n_tok, tokens_loc, targets_loc, up_loc, down_loc, with_top):
    block_len = up_loc.shape[1]
    n_slots = min(4 * n_stage, 2 * n_micro)
    cycle_len = 2 * n_stage
    stage_idx = lax.axis_index("stage")
    fwd_perm = [(src_dev, (src_dev + 1) % n_stage) for src_dev in range(n_stage)]
    bwd_perm = [(src_dev, (src_dev - 1) % n_stage) for src_dev in range(n_stage)]

    def tick(tick_idx, state):
        fwd_in, bwd_in, top_grad, act_stash, acc_list, loss_acc = state
        b_slot = tick_idx - 2 * n_stage - (n_stage - 1 - stage_idx)
        b_valid = (b_slot >= 0) & (b_slot < 2 * n_micro)
        b_slot = jnp.clip(b_slot, 0, 2 * n_micro - 1)
        b_rem = b_slot % cycle_len
        b_virt = 1 - b_rem // n_stage
        b_saved = (b_slot // cycle_len) * cycle_len + b_virt * n_stage + b_rem % n_stage
        saved_pos = b_saved % n_slots
        use_top = (stage_idx == n_stage - 1) & (b_virt == 1)
        g_start = jnp.where(use_top, top_grad, bwd_in)

        def make_bwd(virt_idx):
            acc_pos = 2 * virt_idx

            def run_bwd(operands):
                acc_one = operands[acc_pos]
                acc_two = operands[acc_pos + 1]
                saved_in = lax.dynamic_index_in_dim(act_stash, saved_pos, 0, keepdims=False)
                g_cur = g_start
                for layer_idx in reversed(range(block_len)):
                    g_cur, g_up, g_down = layer_bwd(saved_in[layer_idx], g_cur, up_loc[virt_idx, layer_idx], down_loc[virt_idx, layer_idx])
                    acc_one = add_layer(acc_one, g_up, layer_idx)
                    acc_two = add_layer(acc_two, g_down, layer_idx)
                new_accs = list(operands)
                new_accs[acc_pos] = acc_one
                new_accs[acc_pos + 1] = acc_two
                return tuple(new_accs), g_cur

            return run_bwd

        def skip_bwd(operands):
            return operands, g_start

        branch_list = [skip_bwd, make_bwd(0)] + ([make_bwd(1)] if with_top else [])
        branch_idx = jnp.minimum(jnp.where(b_valid, 1 + b_virt, 0), len(branch_list) - 1)
        acc_list, bwd_out = lax.switch(branch_idx, branch_list, acc_list)

        f_slot = tick_idx - stage_idx
        f_valid = (f_slot >= 0) & (f_slot < 2 * n_micro)
        f_slot = jnp.clip(f_slot, 0, 2 * n_micro - 1)
        f_rem = f_slot % cycle_len
        f_virt = f_rem // n_stage
        f_micro = (f_slot // cycle_len) * n_stage + f_rem % n_stage
        from_data = (stage_idx == 0) & (f_virt == 0)
        h_start = jnp.where(from_data, lax.dynamic_index_in_dim(tokens_loc, f_micro, 0, keepdims=False), fwd_in)
        is_top = (stage_idx == n_stage - 1) & (f_virt == 1)

        def run_fwd(operands):
            stash_cur, loss_cur, top_cur = operands
            w_ones = lax.dynamic_index_in_dim(up_loc, f_virt, 0, keepdims=False)
            w_twos = lax.dynamic_index_in_dim(down_loc, f_virt, 0, keepdims=False)
            h_cur = h_start
            for layer_idx in range(block_len):
                stash_cur = lax.dynamic_update_slice(stash_cur, h_cur[None, None], (f_slot % n_slots, layer_idx, 0, 0))
                h_cur = layer_fwd(h_cur, w_ones[layer_idx], w_twos[layer_idx])
            target_mb = lax.dynamic_index_in_dim(targets_loc, f_micro, 0, keepdims=False)
            out_err = h_cur.astype(jnp.float32) - target_mb.astype(jnp.float32)
            loss_cur = loss_cur + jnp.where(is_top, jnp.sum(out_err * out_err) / (2.0 * n_tok), 0.0)
            top_cur = jnp.where(is_top, (out_err / n_tok).astype(jnp.bfloat16), top_cur)
            return stash_cur, loss_cur, top_cur, h_cur

        def skip_fwd(operands):
            return operands[0], operands[1], operands[2], h_start

        act_stash, loss_acc, top_grad, fwd_out = lax.cond(f_valid, run_fwd, skip_fwd, (act_stash, loss_acc, top_grad))
        fwd_next = lax.ppermute(fwd_out, "stage", fwd_perm)
        bwd_next = lax.ppermute(bwd_out, "stage", bwd_perm)
        return fwd_next, bwd_next, top_grad, act_stash, acc_list, loss_acc

    return tick


def solution(mesh):
    n_stage = mesh.shape["stage"]
    n_data = mesh.shape["data"]

    def device_fn(tokens_loc, targets_loc, up_loc, down_loc):
        n_micro, seq_len, d_model = tokens_loc.shape
        n_tok = n_data * n_micro * seq_len
        block_len = up_loc.shape[1]
        n_slots = min(4 * n_stage, 2 * n_micro)
        zero_act = jnp.zeros((seq_len, d_model), jnp.bfloat16)
        zero_up = jnp.zeros(up_loc.shape[1:], jnp.float32)
        zero_down = jnp.zeros(down_loc.shape[1:], jnp.float32)
        state = (
            zero_act,
            zero_act,
            zero_act,
            jnp.zeros((n_slots, block_len, seq_len, d_model), jnp.bfloat16),
            (zero_up, zero_down, zero_up, zero_down),
            jnp.zeros((), jnp.float32),
        )
        split_tick = 2 * n_micro + 2 * n_stage - 1
        n_ticks = 2 * n_micro + 3 * n_stage - 1
        tick_both = make_tick(n_stage, n_micro, n_tok, tokens_loc, targets_loc, up_loc, down_loc, True)
        fwd_in, bwd_in, top_grad, act_stash, acc_list, loss_acc = lax.fori_loop(0, split_tick, tick_both, state)
        red_up_top = lax.psum_scatter(acc_list[2], "data", scatter_dimension=1, tiled=True)
        red_down_top = lax.psum_scatter(acc_list[3], "data", scatter_dimension=1, tiled=True)
        tick_low = make_tick(n_stage, n_micro, n_tok, tokens_loc, targets_loc, up_loc, down_loc, False)
        state = (fwd_in, bwd_in, top_grad, act_stash, (acc_list[0], acc_list[1]), loss_acc)
        state = lax.fori_loop(split_tick, n_ticks, tick_low, state)
        red_up_low = lax.psum_scatter(state[4][0], "data", scatter_dimension=1, tiled=True)
        red_down_low = lax.psum_scatter(state[4][1], "data", scatter_dimension=1, tiled=True)
        loss = lax.psum(state[5], ("stage", "data"))
        return loss, jnp.stack([red_up_low, red_up_top]), jnp.stack([red_down_low, red_down_top])

    return jax.shard_map(
        device_fn,
        mesh=mesh,
        in_specs=(P("data"), P("data"), P(None, "stage"), P(None, "stage")),
        out_specs=(P(), P(None, "stage", "data"), P(None, "stage", "data")),
        check_vma=False,
    )
```

profile of v0, /device:TPU:0, one launch (start us, length us, event | category | flops | bytes accessed | tf_op | source)
XLA Modules:
  0.0 1702.4 jit_solution(8557953235838918649)
XLA Ops:
  53.1 726.6 %while.62 = (s32[]{:T(128)}, bf16[64,1280]{1,0:T(8,128)(2,1)S(1)}, bf16[64,1280]{1,0:T(8,128)(2,1)S(1)}, bf16[64,1280]{1,0:T(8,128)(2,1)S(1)}, bf16[8,1,64,1280]...) while((s32[]{:T(128)}, bf16[64,1280]{1,0:T(8,128)(2,1)S(1)}, ...), condition=%wide.region_7.8_spmd, body=%wide.region_0.7_spmd.sunk | while | flops 5899796480 | bytes 181210608 | solution.py:141
  279.7 55.9 %collective-permute-start.1 = (bf16[64,1280]{1,0:T(8,128)(2,1)S(1)}, bf16[64,1280]{1,0:T(8,128)(2,1)S(1)}, u32[]{:S(2)}, u32[]{:S(2)}) collective-permute-start(bf16[64,1280]{1,0:T(8,128)(2,1)S(1)} %get-tuple-element.1664), channel_id=1, source_target_pairs={{0,24},{8,0},{16,8},{24,16},{1,25},{9,1},{17,9},{25,17},{2,26},{10... | collective-permute-start | bytes 491528 | tf_op jit(solution)/shard_map/while/body/eval_jaxpr/ppermute | solution.py:112
  338.4 17.5 %collective-permute-done = bf16[64,1280]{1,0:T(8,128)(2,1)S(1)} collective-permute-done((bf16[64,1280]{1,0:T(8,128)(2,1)}, bf16[64,1280]{1,0:T(8,128)(2,1)S(1)}, u32[]{:S(2)}, u32[]{:S(2)}) %collective-permute-start) | collective-permute-done | bytes 163872 | tf_op jit(solution)/shard_map/while/body/eval_jaxpr/ppermute | solution.py:111
  356.9 58.4 %collective-permute-start.1 = (bf16[64,1280]{1,0:T(8,128)(2,1)S(1)}, bf16[64,1280]{1,0:T(8,128)(2,1)S(1)}, u32[]{:S(2)}, u32[]{:S(2)}) collective-permute-start(bf16[64,1280]{1,0:T(8,128)(2,1)S(1)} %get-tuple-element.1664), channel_id=1, source_target_pairs={{0,24},{8,0},{16,8},{24,16},{1,25},{9,1},{17,9},{25,17},{2,26},{10... | collective-permute-start | bytes 491528 | tf_op jit(solution)/shard_map/while/body/eval_jaxpr/ppermute | solution.py:112
  418.1 17.5 %collective-permute-done = bf16[64,1280]{1,0:T(8,128)(2,1)S(1)} collective-permute-done((bf16[64,1280]{1,0:T(8,128)(2,1)}, bf16[64,1280]{1,0:T(8,128)(2,1)S(1)}, u32[]{:S(2)}, u32[]{:S(2)}) %collective-permute-start) | collective-permute-done | bytes 163872 | tf_op jit(solution)/shard_map/while/body/eval_jaxpr/ppermute | solution.py:111
  436.6 58.4 %collective-permute-start.1 = (bf16[64,1280]{1,0:T(8,128)(2,1)S(1)}, bf16[64,1280]{1,0:T(8,128)(2,1)S(1)}, u32[]{:S(2)}, u32[]{:S(2)}) collective-permute-start(bf16[64,1280]{1,0:T(8,128)(2,1)S(1)} %get-tuple-element.1664), channel_id=1, source_target_pairs={{0,24},{8,0},{16,8},{24,16},{1,25},{9,1},{17,9},{25,17},{2,26},{10... | collective-permute-start | bytes 491528 | tf_op jit(solution)/shard_map/while/body/eval_jaxpr/ppermute | solution.py:112
  497.9 17.5 %collective-permute-done = bf16[64,1280]{1,0:T(8,128)(2,1)S(1)} collective-permute-done((bf16[64,1280]{1,0:T(8,128)(2,1)}, bf16[64,1280]{1,0:T(8,128)(2,1)S(1)}, u32[]{:S(2)}, u32[]{:S(2)}) %collective-permute-start) | collective-permute-done | bytes 163872 | tf_op jit(solution)/shard_map/while/body/eval_jaxpr/ppermute | solution.py:111
  516.3 56.4 %conditional.9 = (f32[1,1280,5120]{2,1,0:T(8,128)}, f32[1,5120,1280]{2,1,0:T(8,128)}, f32[1,1280,5120]{2,1,0:T(8,128)}, f32[1,5120,1280]{2,1,0:T(8,128)}, bf16[64,1280]{1,0:T(8,128)(2,1)S(1)}) conditional(s32[]{:T(128)} %clamp.27, (f32[1,1280,5120]{2,1,0:T(8,128)}, f32[1,5120,1280]{2,1,0:T(8,128)}, f32[1,1280,5120]{2,1,0:T(8,128)}, ...), branch_computations={%region_4.4_spmd, %region_5.5_spmd, %region_6.6_spmd} | conditional | flops 4217815040 | bytes 151060544 | solution.py:81
  531.3 17.3 %bitcast_add_fusion.3 = f32[1,1280,5120]{2,1,0:T(8,128)} fusion(f32[1,1280,5120]{2,1,0:T(8,128)} %get-tuple-element.1269, bf16[64,5120]{1,0:T(8,128)(2,1)S(1)} %fusion.107, bf16[8,1,64,1280]{3,2,1,0:T(8,128)(2,1)} %get-tuple-element.1270, s32[]{:T(128)S(6)} %select_n.432), kind=kOutput, calls=%fused_computation.68 | convolution fusion | flops 845414400 | bytes 53248004 | tf_op jit(solution)/shard_map/while/body/eval_jaxpr/cond/branch_2_fun/td,tf->df/dot_general | solution.py:25
  583.5 56.4 %conditional.9 = (f32[1,1280,5120]{2,1,0:T(8,128)}, f32[1,5120,1280]{2,1,0:T(8,128)}, f32[1,1280,5120]{2,1,0:T(8,128)}, f32[1,5120,1280]{2,1,0:T(8,128)}, bf16[64,1280]{1,0:T(8,128)(2,1)S(1)}) conditional(s32[]{:T(128)} %clamp.27, (f32[1,1280,5120]{2,1,0:T(8,128)}, f32[1,5120,1280]{2,1,0:T(8,128)}, f32[1,1280,5120]{2,1,0:T(8,128)}, ...), branch_computations={%region_4.4_spmd, %region_5.5_spmd, %region_6.6_spmd} | conditional | flops 4217815040 | bytes 151060544 | solution.py:81
  648.7 56.4 %conditional.9 = (f32[1,1280,5120]{2,1,0:T(8,128)}, f32[1,5120,1280]{2,1,0:T(8,128)}, f32[1,1280,5120]{2,1,0:T(8,128)}, f32[1,5120,1280]{2,1,0:T(8,128)}, bf16[64,1280]{1,0:T(8,128)(2,1)S(1)}) conditional(s32[]{:T(128)} %clamp.27, (f32[1,1280,5120]{2,1,0:T(8,128)}, f32[1,5120,1280]{2,1,0:T(8,128)}, f32[1,1280,5120]{2,1,0:T(8,128)}, ...), branch_computations={%region_4.4_spmd, %region_5.5_spmd, %region_6.6_spmd} | conditional | flops 4217815040 | bytes 151060544 | solution.py:81
  663.7 17.3 %bitcast_add_fusion.3 = f32[1,1280,5120]{2,1,0:T(8,128)} fusion(f32[1,1280,5120]{2,1,0:T(8,128)} %get-tuple-element.1269, bf16[64,5120]{1,0:T(8,128)(2,1)S(1)} %fusion.107, bf16[8,1,64,1280]{3,2,1,0:T(8,128)(2,1)} %get-tuple-element.1270, s32[]{:T(128)S(6)} %select_n.432), kind=kOutput, calls=%fused_computation.68 | convolution fusion | flops 845414400 | bytes 53248004 | tf_op jit(solution)/shard_map/while/body/eval_jaxpr/cond/branch_2_fun/td,tf->df/dot_general | solution.py:25
  714.7 56.4 %conditional.9 = (f32[1,1280,5120]{2,1,0:T(8,128)}, f32[1,5120,1280]{2,1,0:T(8,128)}, f32[1,1280,5120]{2,1,0:T(8,128)}, f32[1,5120,1280]{2,1,0:T(8,128)}, bf16[64,1280]{1,0:T(8,128)(2,1)S(1)}) conditional(s32[]{:T(128)} %clamp.27, (f32[1,1280,5120]{2,1,0:T(8,128)}, f32[1,5120,1280]{2,1,0:T(8,128)}, f32[1,1280,5120]{2,1,0:T(8,128)}, ...), branch_computations={%region_4.4_spmd, %region_5.5_spmd, %region_6.6_spmd} | conditional | flops 4217815040 | bytes 151060544 | solution.py:81
  729.7 17.3 %bitcast_add_fusion.3 = f32[1,1280,5120]{2,1,0:T(8,128)} fusion(f32[1,1280,5120]{2,1,0:T(8,128)} %get-tuple-element.1269, bf16[64,5120]{1,0:T(8,128)(2,1)S(1)} %fusion.107, bf16[8,1,64,1280]{3,2,1,0:T(8,128)(2,1)} %get-tuple-element.1270, s32[]{:T(128)S(6)} %select_n.432), kind=kOutput, calls=%fused_computation.68 | convolution fusion | flops 845414400 | bytes 53248004 | tf_op jit(solution)/shard_map/while/body/eval_jaxpr/cond/branch_2_fun/td,tf->df/dot_general | solution.py:25
  779.7 262.0 %while.63 = (s32[]{:T(128)}, bf16[64,1280]{1,0:T(8,128)(2,1)S(1)}, bf16[64,1280]{1,0:T(8,128)(2,1)S(1)}, bf16[64,1280]{1,0:T(8,128)(2,1)S(1)}, bf16[8,1,64,1280]...) while((s32[]{:T(128)}, bf16[64,1280]{1,0:T(8,128)(2,1)S(1)}, ...), condition=%wide.region_14.15_spmd, body=%wide.region_8.14_spmd.sunk | while | flops 5899796480 | bytes 181210544 | solution.py:146
  780.7 56.5 %conditional.11 = ((f32[1,1280,5120]{2,1,0:T(8,128)}, f32[1,5120,1280]{2,1,0:T(8,128)}, bf16[64,1280]{1,0:T(8,128)(2,1)S(1)})) conditional(s32[]{:T(128)} %clamp.28, (f32[1,1280,5120]{2,1,0:T(8,128)}, f32[1,5120,1280]{2,1,0:T(8,128)}, bf16[64,1280]{1,0:T(8,128)(2,1)S(1)}) %tuple.153, (s32[]{:T(128)}, s32[]{:T(128)}, s32[]{:T(128)}, ...), branch_computations={%region_12.12_spmd, %region_13.13_spmd} | conditional | flops 4217815040 | bytes 151060832 | solution.py:81
  846.8 56.5 %conditional.11 = ((f32[1,1280,5120]{2,1,0:T(8,128)}, f32[1,5120,1280]{2,1,0:T(8,128)}, bf16[64,1280]{1,0:T(8,128)(2,1)S(1)})) conditional(s32[]{:T(128)} %clamp.28, (f32[1,1280,5120]{2,1,0:T(8,128)}, f32[1,5120,1280]{2,1,0:T(8,128)}, bf16[64,1280]{1,0:T(8,128)(2,1)S(1)}) %tuple.153, (s32[]{:T(128)}, s32[]{:T(128)}, s32[]{:T(128)}, ...), branch_computations={%region_12.12_spmd, %region_13.13_spmd} | conditional | flops 4217815040 | bytes 151060832 | solution.py:81
  912.1 56.5 %conditional.11 = ((f32[1,1280,5120]{2,1,0:T(8,128)}, f32[1,5120,1280]{2,1,0:T(8,128)}, bf16[64,1280]{1,0:T(8,128)(2,1)S(1)})) conditional(s32[]{:T(128)} %clamp.28, (f32[1,1280,5120]{2,1,0:T(8,128)}, f32[1,5120,1280]{2,1,0:T(8,128)}, bf16[64,1280]{1,0:T(8,128)(2,1)S(1)}) %tuple.153, (s32[]{:T(128)}, s32[]{:T(128)}, s32[]{:T(128)}, ...), branch_computations={%region_12.12_spmd, %region_13.13_spmd} | conditional | flops 4217815040 | bytes 151060832 | solution.py:81
  977.4 56.5 %conditional.11 = ((f32[1,1280,5120]{2,1,0:T(8,128)}, f32[1,5120,1280]{2,1,0:T(8,128)}, bf16[64,1280]{1,0:T(8,128)(2,1)S(1)})) conditional(s32[]{:T(128)} %clamp.28, (f32[1,1280,5120]{2,1,0:T(8,128)}, f32[1,5120,1280]{2,1,0:T(8,128)}, bf16[64,1280]{1,0:T(8,128)(2,1)S(1)}) %tuple.153, (s32[]{:T(128)}, s32[]{:T(128)}, s32[]{:T(128)}, ...), branch_computations={%region_12.12_spmd, %region_13.13_spmd} | conditional | flops 4217815040 | bytes 151060832 | solution.py:81
  1043.8 39.5 %psum.7 = f32[]{:T(128)} all-reduce(f32[]{:T(128)} %get-tuple-element.1370), channel_id=1, replica_groups=mesh['stage'=4,'data'=8] {'stage','data'}, use_global_device_ids=true, to_apply=%region_15.16 | all-reduce | flops 1 | bytes 8 | tf_op jit(solution)/shard_map/psum | solution.py:149
  1083.4 116.2 %reduce-scatter.9.cloned.1.call-done = f32[1,640,1280]{2,1,0:T(8,128)} async-done(((f32[1,5120,1280]{2,1,0:T(8,128)}), f32[1,640,1280]{2,1,0:T(8,128)}) %reduce-scatter.9.cloned.1.call-update) | async-done | bytes 3276816 | tf_op jit(solution)/shard_map/reduce_scatter | solution.py:148
  1199.6 163.2 %reduce-scatter.11.cloned.1.call-done = f32[1,640,1280]{2,1,0:T(8,128)} async-done(((f32[1,5120,1280]{2,1,0:T(8,128)}), f32[1,640,1280]{2,1,0:T(8,128)}) %reduce-scatter.11.cloned.1.call-update) | async-done | bytes 3276816 | tf_op jit(solution)/shard_map/reduce_scatter | solution.py:143
  1368.9 157.1 %reduce-scatter.5.cloned.1.call-done = f32[1,160,5120]{2,1,0:T(8,128)} async-done(((f32[1,1280,5120]{2,1,0:T(8,128)}), f32[1,160,5120]{2,1,0:T(8,128)}) %reduce-scatter.5.cloned.1.call-update) | async-done | bytes 3276816 | tf_op jit(solution)/shard_map/reduce_scatter | solution.py:147
  1526.0 163.0 %reduce-scatter.7.cloned.1.call-done = f32[1,160,5120]{2,1,0:T(8,128)} async-done(((f32[1,1280,5120]{2,1,0:T(8,128)}), f32[1,160,5120]{2,1,0:T(8,128)}) %reduce-scatter.7.cloned.1.call-update) | async-done | bytes 3276816 | tf_op jit(solution)/shard_map/reduce_scatter | solution.py:142
  (222 shorter events, 895.5 us)
Async XLA Ops:
  7.2 1192.4 %reduce-scatter.9.cloned.1.call-start = ((), (), s32[]{:S(2)}) async-start(), calls=%async_computation.6 | async-start | bytes 29491200 | tf_op jit(solution)/shard_map/reduce_scatter | solution.py:148
  67.8 22.2 %collective-permute-start.1 = (bf16[64,1280]{1,0:T(8,128)(2,1)S(1)}, bf16[64,1280]{1,0:T(8,128)(2,1)S(1)}, u32[]{:S(2)}, u32[]{:S(2)}) collective-permute-start(bf16[64,1280]{1,0:T(8,128)(2,1)S(1)} %get-tuple-element.1664), channel_id=1, source_target_pairs={{0,24},{8,0},{16,8},{24,16},{1,25},{9,1},{17,9},{25,17},{2,26},{10... | collective-permute-start | bytes 491528 | tf_op jit(solution)/shard_map/while/body/eval_jaxpr/ppermute | solution.py:112
  89.9 8.9 collective-permute-start
  99.8 19.1 %collective-permute-start.1 = (bf16[64,1280]{1,0:T(8,128)(2,1)S(1)}, bf16[64,1280]{1,0:T(8,128)(2,1)S(1)}, u32[]{:S(2)}, u32[]{:S(2)}) collective-permute-start(bf16[64,1280]{1,0:T(8,128)(2,1)S(1)} %get-tuple-element.1664), channel_id=1, source_target_pairs={{0,24},{8,0},{16,8},{24,16},{1,25},{9,1},{17,9},{25,17},{2,26},{10... | collective-permute-start | bytes 491528 | tf_op jit(solution)/shard_map/while/body/eval_jaxpr/ppermute | solution.py:112
  116.8 8.2 collective-permute-start
  126.1 19.1 %collective-permute-start.1 = (bf16[64,1280]{1,0:T(8,128)(2,1)S(1)}, bf16[64,1280]{1,0:T(8,128)(2,1)S(1)}, u32[]{:S(2)}, u32[]{:S(2)}) collective-permute-start(bf16[64,1280]{1,0:T(8,128)(2,1)S(1)} %get-tuple-element.1664), channel_id=1, source_target_pairs={{0,24},{8,0},{16,8},{24,16},{1,25},{9,1},{17,9},{25,17},{2,26},{10... | collective-permute-start | bytes 491528 | tf_op jit(solution)/shard_map/while/body/eval_jaxpr/ppermute | solution.py:112
  143.2 7.4 collective-permute-start
  151.6 19.1 %collective-permute-start.1 = (bf16[64,1280]{1,0:T(8,128)(2,1)S(1)}, bf16[64,1280]{1,0:T(8,128)(2,1)S(1)}, u32[]{:S(2)}, u32[]{:S(2)}) collective-permute-start(bf16[64,1280]{1,0:T(8,128)(2,1)S(1)} %get-tuple-element.1664), channel_id=1, source_target_pairs={{0,24},{8,0},{16,8},{24,16},{1,25},{9,1},{17,9},{25,17},{2,26},{10... | collective-permute-start | bytes 491528 | tf_op jit(solution)/shard_map/while/body/eval_jaxpr/ppermute | solution.py:112
  168.7 7.2 collective-permute-start
  176.9 19.1 %collective-permute-start.1 = (bf16[64,1280]{1,0:T(8,128)(2,1)S(1)}, bf16[64,1280]{1,0:T(8,128)(2,1)S(1)}, u32[]{:S(2)}, u32[]{:S(2)}) collective-permute-start(bf16[64,1280]{1,0:T(8,128)(2,1)S(1)} %get-tuple-element.1664), channel_id=1, source_target_pairs={{0,24},{8,0},{16,8},{24,16},{1,25},{9,1},{17,9},{25,17},{2,26},{10... | collective-permute-start | bytes 491528 | tf_op jit(solution)/shard_map/while/body/eval_jaxpr/ppermute | solution.py:112
  203.9 19.1 %collective-permute-start.1 = (bf16[64,1280]{1,0:T(8,128)(2,1)S(1)}, bf16[64,1280]{1,0:T(8,128)(2,1)S(1)}, u32[]{:S(2)}, u32[]{:S(2)}) collective-permute-start(bf16[64,1280]{1,0:T(8,128)(2,1)S(1)} %get-tuple-element.1664), channel_id=1, source_target_pairs={{0,24},{8,0},{16,8},{24,16},{1,25},{9,1},{17,9},{25,17},{2,26},{10... | collective-permute-start | bytes 491528 | tf_op jit(solution)/shard_map/while/body/eval_jaxpr/ppermute | solution.py:112
  221.0 7.2 collective-permute-start
  229.2 19.1 %collective-permute-start.1 = (bf16[64,1280]{1,0:T(8,128)(2,1)S(1)}, bf16[64,1280]{1,0:T(8,128)(2,1)S(1)}, u32[]{:S(2)}, u32[]{:S(2)}) collective-permute-start(bf16[64,1280]{1,0:T(8,128)(2,1)S(1)} %get-tuple-element.1664), channel_id=1, source_target_pairs={{0,24},{8,0},{16,8},{24,16},{1,25},{9,1},{17,9},{25,17},{2,26},{10... | collective-permute-start | bytes 491528 | tf_op jit(solution)/shard_map/while/body/eval_jaxpr/ppermute | solution.py:112
  246.2 7.2 collective-permute-start
  254.4 19.1 %collective-permute-start.1 = (bf16[64,1280]{1,0:T(8,128)(2,1)S(1)}, bf16[64,1280]{1,0:T(8,128)(2,1)S(1)}, u32[]{:S(2)}, u32[]{:S(2)}) collective-permute-start(bf16[64,1280]{1,0:T(8,128)(2,1)S(1)} %get-tuple-element.1664), channel_id=1, source_target_pairs={{0,24},{8,0},{16,8},{24,16},{1,25},{9,1},{17,9},{25,17},{2,26},{10... | collective-permute-start | bytes 491528 | tf_op jit(solution)/shard_map/while/body/eval_jaxpr/ppermute | solution.py:112
  279.7 58.7 %collective-permute-start.1 = (bf16[64,1280]{1,0:T(8,128)(2,1)S(1)}, bf16[64,1280]{1,0:T(8,128)(2,1)S(1)}, u32[]{:S(2)}, u32[]{:S(2)}) collective-permute-start(bf16[64,1280]{1,0:T(8,128)(2,1)S(1)} %get-tuple-element.1664), channel_id=1, source_target_pairs={{0,24},{8,0},{16,8},{24,16},{1,25},{9,1},{17,9},{25,17},{2,26},{10... | collective-permute-start | bytes 491528 | tf_op jit(solution)/shard_map/while/body/eval_jaxpr/ppermute | solution.py:112
  336.2 19.6 %collective-permute-start = (bf16[64,1280]{1,0:T(8,128)(2,1)}, bf16[64,1280]{1,0:T(8,128)(2,1)S(1)}, u32[]{:S(2)}, u32[]{:S(2)}) collective-permute-start(bf16[64,1280]{1,0:T(8,128)(2,1)} %get-tuple-element.1662), channel_id=1, source_target_pairs={{0,8},{8,16},{16,24},{24,0},{1,9},{9,17},{17,25},{25,1},{2,10},{10... | collective-permute-start | bytes 491528 | tf_op jit(solution)/shard_map/while/body/eval_jaxpr/ppermute | solution.py:111
  356.9 61.2 %collective-permute-start.1 = (bf16[64,1280]{1,0:T(8,128)(2,1)S(1)}, bf16[64,1280]{1,0:T(8,128)(2,1)S(1)}, u32[]{:S(2)}, u32[]{:S(2)}) collective-permute-start(bf16[64,1280]{1,0:T(8,128)(2,1)S(1)} %get-tuple-element.1664), channel_id=1, source_target_pairs={{0,24},{8,0},{16,8},{24,16},{1,25},{9,1},{17,9},{25,17},{2,26},{10... | collective-permute-start | bytes 491528 | tf_op jit(solution)/shard_map/while/body/eval_jaxpr/ppermute | solution.py:112
  416.0 19.6 %collective-permute-start = (bf16[64,1280]{1,0:T(8,128)(2,1)}, bf16[64,1280]{1,0:T(8,128)(2,1)S(1)}, u32[]{:S(2)}, u32[]{:S(2)}) collective-permute-start(bf16[64,1280]{1,0:T(8,128)(2,1)} %get-tuple-element.1662), channel_id=1, source_target_pairs={{0,8},{8,16},{16,24},{24,0},{1,9},{9,17},{17,25},{25,1},{2,10},{10... | collective-permute-start | bytes 491528 | tf_op jit(solution)/shard_map/while/body/eval_jaxpr/ppermute | solution.py:111
  436.6 61.2 %collective-permute-start.1 = (bf16[64,1280]{1,0:T(8,128)(2,1)S(1)}, bf16[64,1280]{1,0:T(8,128)(2,1)S(1)}, u32[]{:S(2)}, u32[]{:S(2)}) collective-permute-start(bf16[64,1280]{1,0:T(8,128)(2,1)S(1)} %get-tuple-element.1664), channel_id=1, source_target_pairs={{0,24},{8,0},{16,8},{24,16},{1,25},{9,1},{17,9},{25,17},{2,26},{10... | collective-permute-start | bytes 491528 | tf_op jit(solution)/shard_map/while/body/eval_jaxpr/ppermute | solution.py:112
  495.7 19.6 %collective-permute-start = (bf16[64,1280]{1,0:T(8,128)(2,1)}, bf16[64,1280]{1,0:T(8,128)(2,1)S(1)}, u32[]{:S(2)}, u32[]{:S(2)}) collective-permute-start(bf16[64,1280]{1,0:T(8,128)(2,1)} %get-tuple-element.1662), channel_id=1, source_target_pairs={{0,8},{8,16},{16,24},{24,0},{1,9},{9,17},{17,25},{25,1},{2,10},{10... | collective-permute-start | bytes 491528 | tf_op jit(solution)/shard_map/while/body/eval_jaxpr/ppermute | solution.py:111
  1041.8 321.0 %reduce-scatter.11.cloned.1.call-start = ((), (), s32[]{:S(2)}) async-start(), calls=%async_computation.7 | async-start | bytes 29491200 | tf_op jit(solution)/shard_map/reduce_scatter | solution.py:143
  1042.5 483.5 %reduce-scatter.5.cloned.1.call-start = ((), (), s32[]{:S(2)}) async-start(), calls=%async_computation.4 | async-start | bytes 29491200 | tf_op jit(solution)/shard_map/reduce_scatter | solution.py:147
  1043.3 645.8 %reduce-scatter.7.cloned.1.call-start = ((), (), s32[]{:S(2)}) async-start(), calls=%async_computation.5 | async-start | bytes 29491200 | tf_op jit(solution)/shard_map/reduce_scatter | solution.py:142
  (19 other events, 115.4 us)
Sparse Core Ops, SparseCore 0:
  1041.9 157.6 reduce-scatter.8
  1203.3 159.4 reduce-scatter.10
  1366.5 159.4 reduce-scatter.4
  1529.5 159.4 reduce-scatter.6
where the time goes:
time: 1710 us; the launch traced here: 1700 us
  waiting for transfers between devices  754 us (44%)
  matrix products  568 us (33%)
  starting transfers between devices  209 us (12%)
  local copies, waits for them, and re-layouts  58.8 us (3%)
  blocking collectives  39.5 us (2%)
  other arithmetic  38.7 us (2%)
  loops' own time  20.2 us (1%)
    ppermute x19, starting transfers between devices, tick(): bwd_next = lax.ppermute(bwd_out, 'stage', bwd_perm)  185 us
    reduce_scatter x1, waiting for transfers between devices, device_fn(): lax.psum_scatter(acc_list[3], 'data', scatter_dimension=1, tiled=True)  163 us
    reduce_scatter x1, waiting for transfers between devices, device_fn(): lax.psum_scatter(acc_list[2], 'data', scatter_dimension=1, tiled=True)  163 us
    reduce_scatter x1, waiting for transfers between devices, device_fn(): lax.psum_scatter(state[4][0], 'data', scatter_dimension=1, tiled=True)  157 us
    dot_general x8, matrix products, layer_bwd(): jnp.einsum('td,tf->df', h_in, d_pre, preferred_element_type=jnp.float32)  138 us
    dot_general x8, matrix products, layer_bwd(): jnp.einsum('tf,td->fd', act_bf, grad_out, preferred_element_type=jnp.floa...  136 us
    ppermute x19, waiting for transfers between devices, tick(): fwd_next = lax.ppermute(fwd_out, 'stage', fwd_perm)  125 us
    dot_general x8, matrix products, layer_fwd(): jnp.dot(act_bf, w_two, preferred_element_type=jnp.float32)  117 us
  transfers between devices with their start and end apart: 42, of which 34 were waited for; matrix products, arithmetic and copies ran while one was open for 8% of the time, Pallas kernels for 0%

commit v1 on v0

v1 whole, which is shorter than its diff:
```python
import jax
import jax.numpy as jnp
from jax import lax
from jax.sharding import PartitionSpec as P


def gelu_fn(pre_act):
    return jax.nn.gelu(pre_act, approximate=True)


def matmul(lhs, rhs, dims):
    return lax.dot_general(lhs, rhs, (dims, ((), ())), preferred_element_type=jnp.float32)


def layer_fwd(h_in, w_one, w_two):
    act = gelu_fn(matmul(h_in, w_one, ((1,), (0,)))).astype(jnp.bfloat16)
    out_val = h_in.astype(jnp.float32) + matmul(act, w_two, ((1,), (0,)))
    return out_val.astype(jnp.bfloat16)


def act_bwd(h_in, grad_out, w_one, w_two):
    pre_act = matmul(h_in, w_one, ((1,), (0,)))
    act_val, gelu_vjp = jax.vjp(gelu_fn, pre_act)
    d_act = matmul(grad_out, w_two, ((1,), (1,))).astype(jnp.bfloat16)
    d_pre = gelu_vjp(d_act.astype(jnp.float32))[0].astype(jnp.bfloat16)
    return act_val.astype(jnp.bfloat16), d_pre


def layer_dgrad(h_in, grad_out, w_one, w_two):
    _, d_pre = act_bwd(h_in, grad_out, w_one, w_two)
    back_val = matmul(d_pre, w_one, ((1,), (1,)))
    return (grad_out.astype(jnp.float32) + back_val).astype(jnp.bfloat16)


def put_slot(buf, val, idx):
    return lax.dynamic_update_slice(buf, val[None], (idx, 0, 0))


def solution(mesh):
    n_stage = mesh.shape["stage"]
    n_data = mesh.shape["data"]

    def device_fn(tokens_loc, targets_loc, up_loc, down_loc):
        n_micro, seq_len, d_model = tokens_loc.shape
        d_ff = up_loc.shape[3]
        n_tok = n_data * n_micro * seq_len
        n_slots = 2 * n_micro
        stage_idx = lax.axis_index("stage")
        data_idx = lax.axis_index("data")
        is_first = stage_idx == 0
        is_last = stage_idx == n_stage - 1
        fwd_perm = [(src, (src + 1) % n_stage) for src in range(n_stage)]
        bwd_perm = [(src, (src - 1) % n_stage) for src in range(n_stage)]
        up_loc = up_loc[:, 0]
        down_loc = down_loc[:, 0]

        def pick(arr, idx):
            return lax.dynamic_index_in_dim(arr, idx, 0, keepdims=False)

        def fwd_slot(tick_idx, state):
            h_in, stash, tops, loss = state
            slot = tick_idx - stage_idx
            valid = (slot >= 0) & (slot < n_slots)
            slot = jnp.clip(slot, 0, n_slots - 1)
            virt = slot // n_micro
            micro = slot % n_micro
            h_cur = jnp.where(is_first & (virt == 0), pick(tokens_loc, micro), h_in)
            stash = put_slot(stash, h_cur, jnp.where(valid, slot, n_slots))
            h_out = layer_fwd(h_cur, pick(up_loc, virt), pick(down_loc, virt))
            err = h_out.astype(jnp.float32) - pick(targets_loc, micro).astype(jnp.float32)
            is_top = is_last & valid & (virt == 1)
            loss = loss + jnp.where(is_top, jnp.sum(err * err) / (2.0 * n_tok), 0.0)
            tops = put_slot(tops, (err / n_tok).astype(jnp.bfloat16), jnp.where(is_top, micro, n_micro))
            return lax.ppermute(h_out, "stage", fwd_perm), stash, tops, loss

        def bwd_slot(tick_idx, state):
            g_in, gstash = state
            slot = tick_idx - (n_stage - 1 - stage_idx)
            valid = (slot >= 0) & (slot < n_slots)
            slot = jnp.clip(slot, 0, n_slots - 1)
            virt = 1 - slot // n_micro
            micro = slot % n_micro
            g_cur = jnp.where(is_last & (virt == 1), pick(tops, micro), g_in)
            pos = virt * n_micro + micro
            gstash = put_slot(gstash, g_cur, jnp.where(valid, pos, n_slots))
            g_out = layer_dgrad(pick(stash, pos), g_cur, pick(up_loc, virt), pick(down_loc, virt))
            return lax.ppermute(g_out, "stage", bwd_perm), gstash

        n_ticks = n_slots + n_stage - 1
        zero_act = jnp.zeros((seq_len, d_model), jnp.bfloat16)
        stash0 = jnp.zeros((n_slots + 1, seq_len, d_model), jnp.bfloat16)
        tops0 = jnp.zeros((n_micro + 1, seq_len, d_model), jnp.bfloat16)
        _, stash, tops, loss = lax.fori_loop(0, n_ticks, fwd_slot, (zero_act, stash0, tops0, jnp.zeros((), jnp.float32)))
        _, gstash = lax.fori_loop(0, n_ticks, bwd_slot, (zero_act, stash0))

        f_loc = d_ff // n_data
        ups, downs = [], []
        for virt in range(2):
            h_all = lax.all_gather(stash[virt * n_micro:(virt + 1) * n_micro].reshape(-1, d_model), "data", tiled=True)
            g_all = lax.all_gather(gstash[virt * n_micro:(virt + 1) * n_micro].reshape(-1, d_model), "data", tiled=True)
            w_one = lax.dynamic_slice(up_loc[virt], (0, data_idx * f_loc), (d_model, f_loc))
            w_two = lax.dynamic_slice(down_loc[virt], (data_idx * f_loc, 0), (f_loc, d_model))
            act, d_pre = act_bwd(h_all, g_all, w_one, w_two)
            downs.append(matmul(act, g_all, ((0,), (0,))))
            g_up = matmul(h_all, d_pre, ((0,), (0,)))
            ups.append(lax.all_to_all(g_up, "data", 0, 1, tiled=True))
        loss = lax.psum(loss, ("stage", "data"))
        return loss, jnp.stack(ups)[:, None], jnp.stack(downs)[:, None]

    return jax.shard_map(
        device_fn,
        mesh=mesh,
        in_specs=(P("data"), P("data"), P(None, "stage"), P(None, "stage")),
        out_specs=(P(), P(None, "stage", "data"), P(None, "stage", "data")),
        check_vma=False,
    )
```

time: 1710 us -> 851 us (0.50)
  waiting for transfers between devices: 754 us -> 114 us
  starting transfers between devices: 209 us -> 54.2 us
  matrix products: 568 us -> 465 us
  blocking collectives: 39.5 us -> 73.1 us
    reduce_scatter x4 -> x0, waiting for transfers between devices: 600 us -> none  [the longest x1 163 us: device_fn(): lax.psum_scatter(acc_list[3], 'data', scatter_dimension=1, tiled=True)]
    ppermute x38 -> x22, starting transfers between devices: 209 us -> 45.8 us  [the longest x11 42.1 us: bwd_slot(): return (lax.ppermute(g_out, 'stage', bwd_perm), gstash)]
    dot_general x48 -> x39, matrix products: 568 us -> 465 us  [matmul(): lax.dot_general(lhs, rhs, (dims, ((), ())), preferred_element_type=jnp.fl...]
    ppermute x38 -> x22, waiting for transfers between devices: 152 us -> 60.5 us  [the longest x11 35.1 us: fwd_slot(): return (lax.ppermute(h_out, 'stage', fwd_perm), stash, tops, loss)]
    all_gather x0 -> x4, waiting for transfers between devices: none -> 52 us  [the longest x2 52 us: device_fn(): lax.all_gather(gstash[virt * n_micro:(virt + 1) * n_micro].reshape(-1, d_...]
    broadcast_in_dim x5 -> x3, local copies, waits for them, and re-layouts: 45.7 us -> 2.51 us  [the longest x2 2.46 us: device_fn(): stash0 = jnp.zeros((n_slots + 1, seq_len, d_model), jnp.bfloat16)]
    slice x0 -> x4, local copies, waits for them, and re-layouts: none -> 42.3 us  [the longest x1 19.6 us: device_fn(): up_loc[virt]]
    psum x1, blocking collectives: 39.5 us -> 73.1 us  [device_fn(): loss = lax.psum(loss, ('stage', 'data'))]
  transfers between devices with their start and end apart: 42 -> 28, of which waited for: 34 -> 23; matrix products, arithmetic and copies ran while one was open for 8% -> 49% of each run, Pallas kernels for 0% -> 0%
where the time goes in v1:
time: 851 us; the launch traced here: 843 us
  matrix products  465 us (55%)
  waiting for transfers between devices  114 us (13%)
  blocking collectives  73.1 us (9%)
  local copies, waits for them, and re-layouts  61.8 us (7%)
  starting transfers between devices  54.2 us (6%)
  other arithmetic  51.9 us (6%)
  between operations  14.1 us (2%)
  loops' own time  8.67 us (1%)
    dot_general x39, matrix products, matmul(): lax.dot_general(lhs, rhs, (dims, ((), ())), preferred_element_type=jnp.fl...  465 us
    psum x1, blocking collectives, device_fn(): loss = lax.psum(loss, ('stage', 'data'))  73.1 us
    all_gather x2, waiting for transfers between devices, device_fn(): lax.all_gather(gstash[virt * n_micro:(virt + 1) * n_micro].reshape(-1, d_...  52 us
    ppermute x11, starting transfers between devices, bwd_slot(): return (lax.ppermute(g_out, 'stage', bwd_perm), gstash)  42.1 us
    ppermute x11, waiting for transfers between devices, fwd_slot(): return (lax.ppermute(h_out, 'stage', fwd_perm), stash, tops, loss)  35.1 us
    dynamic_update_slice x22, other arithmetic, put_slot(): return lax.dynamic_update_slice(buf, val[None], (idx, 0, 0))  25.7 us
    ppermute x11, waiting for transfers between devices, bwd_slot(): return (lax.ppermute(g_out, 'stage', bwd_perm), gstash)  25.3 us
    slice x1, local copies, waits for them, and re-layouts, device_fn(): up_loc[virt]  19.6 us
  transfers between devices with their start and end apart: 28, of which 23 were waited for; matrix products, arithmetic and copies ran while one was open for 49% of the time, Pallas kernels for 0%

profile of v1, /device:TPU:0, one launch (start us, length us, event | category | flops | bytes accessed | tf_op | source)
XLA Modules:
  0.0 842.7 jit_solution(11666068754984450295)
XLA Ops:
  8.5 230.6 %while.38 = (s32[]{:T(128)}, bf16[64,1280]{1,0:T(8,128)(2,1)S(1)}, bf16[9,64,1280]{2,1,0:T(8,128)(2,1)}, bf16[5,64,1280]{2,1,0:T(8,128)(2,1)S(1)}, f32[]{:T(128)...) while((s32[]{:T(128)}, bf16[64,1280]{1,0:T(8,128)(2,1)S(1)}, ...), condition=%wide.region_2.3_spmd, body=%wide.region_0.2_spmd.sunk | while | flops 1681981440 | bytes 29167728 | solution.py:93
  8.6 13.4 %fusion.181 = (bf16[5,64,1280]{2,1,0:T(8,128)(2,1)S(1)}, bf16[64,1280]{1,0:T(8,128)(2,1)S(1)}) fusion(bf16[5,64,1280]{2,1,0:T(8,128)(2,1)S(1)} %get-tuple-element.738, s32[]{:T(128)S(6)} %select_n.298, bf16[4,64,1280]{2,1,0:T(8,128)(2,1)} %get-tuple-element.768, s32[]{:T(128)S(6)} %select_n.299, bf16[2,5120,1280]{2,1,0:T(8,128)(2,1)} %get-tuple-element.767, ...), kind=kOutput, calls=%fused_computation.21.clone.1 | convolution fusion | flops 1681489920 | bytes 27364864 | tf_op jit(solution)/shard_map/while/body/eval_jaxpr/dot_general | solution.py:12
  32.1 13.4 %fusion.181 = (bf16[5,64,1280]{2,1,0:T(8,128)(2,1)S(1)}, bf16[64,1280]{1,0:T(8,128)(2,1)S(1)}) fusion(bf16[5,64,1280]{2,1,0:T(8,128)(2,1)S(1)} %get-tuple-element.738, s32[]{:T(128)S(6)} %select_n.298, bf16[4,64,1280]{2,1,0:T(8,128)(2,1)} %get-tuple-element.768, s32[]{:T(128)S(6)} %select_n.299, bf16[2,5120,1280]{2,1,0:T(8,128)(2,1)} %get-tuple-element.767, ...), kind=kOutput, calls=%fused_computation.21.clone.1 | convolution fusion | flops 1681489920 | bytes 27364864 | tf_op jit(solution)/shard_map/while/body/eval_jaxpr/dot_general | solution.py:12
  52.8 13.4 %fusion.181 = (bf16[5,64,1280]{2,1,0:T(8,128)(2,1)S(1)}, bf16[64,1280]{1,0:T(8,128)(2,1)S(1)}) fusion(bf16[5,64,1280]{2,1,0:T(8,128)(2,1)S(1)} %get-tuple-element.738, s32[]{:T(128)S(6)} %select_n.298, bf16[4,64,1280]{2,1,0:T(8,128)(2,1)} %get-tuple-element.768, s32[]{:T(128)S(6)} %select_n.299, bf16[2,5120,1280]{2,1,0:T(8,128)(2,1)} %get-tuple-element.767, ...), kind=kOutput, calls=%fused_computation.21.clone.1 | convolution fusion | flops 1681489920 | bytes 27364864 | tf_op jit(solution)/shard_map/while/body/eval_jaxpr/dot_general | solution.py:12
  73.4 13.4 %fusion.181 = (bf16[5,64,1280]{2,1,0:T(8,128)(2,1)S(1)}, bf16[64,1280]{1,0:T(8,128)(2,1)S(1)}) fusion(bf16[5,64,1280]{2,1,0:T(8,128)(2,1)S(1)} %get-tuple-element.738, s32[]{:T(128)S(6)} %select_n.298, bf16[4,64,1280]{2,1,0:T(8,128)(2,1)} %get-tuple-element.768, s32[]{:T(128)S(6)} %select_n.299, bf16[2,5120,1280]{2,1,0:T(8,128)(2,1)} %get-tuple-element.767, ...), kind=kOutput, calls=%fused_computation.21.clone.1 | convolution fusion | flops 1681489920 | bytes 27364864 | tf_op jit(solution)/shard_map/while/body/eval_jaxpr/dot_general | solution.py:12
  94.1 13.4 %fusion.181 = (bf16[5,64,1280]{2,1,0:T(8,128)(2,1)S(1)}, bf16[64,1280]{1,0:T(8,128)(2,1)S(1)}) fusion(bf16[5,64,1280]{2,1,0:T(8,128)(2,1)S(1)} %get-tuple-element.738, s32[]{:T(128)S(6)} %select_n.298, bf16[4,64,1280]{2,1,0:T(8,128)(2,1)} %get-tuple-element.768, s32[]{:T(128)S(6)} %select_n.299, bf16[2,5120,1280]{2,1,0:T(8,128)(2,1)} %get-tuple-element.767, ...), kind=kOutput, calls=%fused_computation.21.clone.1 | convolution fusion | flops 1681489920 | bytes 27364864 | tf_op jit(solution)/shard_map/while/body/eval_jaxpr/dot_general | solution.py:12
  114.8 13.4 %fusion.181 = (bf16[5,64,1280]{2,1,0:T(8,128)(2,1)S(1)}, bf16[64,1280]{1,0:T(8,128)(2,1)S(1)}) fusion(bf16[5,64,1280]{2,1,0:T(8,128)(2,1)S(1)} %get-tuple-element.738, s32[]{:T(128)S(6)} %select_n.298, bf16[4,64,1280]{2,1,0:T(8,128)(2,1)} %get-tuple-element.768, s32[]{:T(128)S(6)} %select_n.299, bf16[2,5120,1280]{2,1,0:T(8,128)(2,1)} %get-tuple-element.767, ...), kind=kOutput, calls=%fused_computation.21.clone.1 | convolution fusion | flops 1681489920 | bytes 27364864 | tf_op jit(solution)/shard_map/while/body/eval_jaxpr/dot_general | solution.py:12
  135.5 13.4 %fusion.181 = (bf16[5,64,1280]{2,1,0:T(8,128)(2,1)S(1)}, bf16[64,1280]{1,0:T(8,128)(2,1)S(1)}) fusion(bf16[5,64,1280]{2,1,0:T(8,128)(2,1)S(1)} %get-tuple-element.738, s32[]{:T(128)S(6)} %select_n.298, bf16[4,64,1280]{2,1,0:T(8,128)(2,1)} %get-tuple-element.768, s32[]{:T(128)S(6)} %select_n.299, bf16[2,5120,1280]{2,1,0:T(8,128)(2,1)} %get-tuple-element.767, ...), kind=kOutput, calls=%fused_computation.21.clone.1 | convolution fusion | flops 1681489920 | bytes 27364864 | tf_op jit(solution)/shard_map/while/body/eval_jaxpr/dot_general | solution.py:12
  156.2 13.5 %fusion.181 = (bf16[5,64,1280]{2,1,0:T(8,128)(2,1)S(1)}, bf16[64,1280]{1,0:T(8,128)(2,1)S(1)}) fusion(bf16[5,64,1280]{2,1,0:T(8,128)(2,1)S(1)} %get-tuple-element.738, s32[]{:T(128)S(6)} %select_n.298, bf16[4,64,1280]{2,1,0:T(8,128)(2,1)} %get-tuple-element.768, s32[]{:T(128)S(6)} %select_n.299, bf16[2,5120,1280]{2,1,0:T(8,128)(2,1)} %get-tuple-element.767, ...), kind=kOutput, calls=%fused_computation.21.clone.1 | convolution fusion | flops 1681489920 | bytes 27364864 | tf_op jit(solution)/shard_map/while/body/eval_jaxpr/dot_general | solution.py:12
  176.9 13.5 %fusion.181 = (bf16[5,64,1280]{2,1,0:T(8,128)(2,1)S(1)}, bf16[64,1280]{1,0:T(8,128)(2,1)S(1)}) fusion(bf16[5,64,1280]{2,1,0:T(8,128)(2,1)S(1)} %get-tuple-element.738, s32[]{:T(128)S(6)} %select_n.298, bf16[4,64,1280]{2,1,0:T(8,128)(2,1)} %get-tuple-element.768, s32[]{:T(128)S(6)} %select_n.299, bf16[2,5120,1280]{2,1,0:T(8,128)(2,1)} %get-tuple-element.767, ...), kind=kOutput, calls=%fused_computation.21.clone.1 | convolution fusion | flops 1681489920 | bytes 27364864 | tf_op jit(solution)/shard_map/while/body/eval_jaxpr/dot_general | solution.py:12
  197.7 13.5 %fusion.181 = (bf16[5,64,1280]{2,1,0:T(8,128)(2,1)S(1)}, bf16[64,1280]{1,0:T(8,128)(2,1)S(1)}) fusion(bf16[5,64,1280]{2,1,0:T(8,128)(2,1)S(1)} %get-tuple-element.738, s32[]{:T(128)S(6)} %select_n.298, bf16[4,64,1280]{2,1,0:T(8,128)(2,1)} %get-tuple-element.768, s32[]{:T(128)S(6)} %select_n.299, bf16[2,5120,1280]{2,1,0:T(8,128)(2,1)} %get-tuple-element.767, ...), kind=kOutput, calls=%fused_computation.21.clone.1 | convolution fusion | flops 1681489920 | bytes 27364864 | tf_op jit(solution)/shard_map/while/body/eval_jaxpr/dot_general | solution.py:12
  218.4 13.5 %fusion.181 = (bf16[5,64,1280]{2,1,0:T(8,128)(2,1)S(1)}, bf16[64,1280]{1,0:T(8,128)(2,1)S(1)}) fusion(bf16[5,64,1280]{2,1,0:T(8,128)(2,1)S(1)} %get-tuple-element.738, s32[]{:T(128)S(6)} %select_n.298, bf16[4,64,1280]{2,1,0:T(8,128)(2,1)} %get-tuple-element.768, s32[]{:T(128)S(6)} %select_n.299, bf16[2,5120,1280]{2,1,0:T(8,128)(2,1)} %get-tuple-element.767, ...), kind=kOutput, calls=%fused_computation.21.clone.1 | convolution fusion | flops 1681489920 | bytes 27364864 | tf_op jit(solution)/shard_map/while/body/eval_jaxpr/dot_general | solution.py:12
  242.9 297.9 %while.39 = (s32[]{:T(128)}, bf16[64,1280]{1,0:T(8,128)(2,1)S(1)}, bf16[9,64,1280]{2,1,0:T(8,128)(2,1)}, s32[]{:T(128)}, pred[]{:T(512)}, /*index=5*/bf16[5,64,1...) while((s32[]{:T(128)}, bf16[64,1280]{1,0:T(8,128)(2,1)S(1)}, ...), condition=%wide.region_5.6_spmd, body=%wide.region_4.5_spmd.sunk | while | flops 2524282880 | bytes 44404304 | solution.py:94
  328.7 13.0 %fusion.187 = bf16[64,1280]{1,0:T(8,128)(2,1)S(1)} fusion(bf16[2,1280,5120]{2,1,0:T(8,128)(2,1)} %get-tuple-element.827, s32[]{:T(128)S(6)} %select_n.310, f32[64,5120]{1,0:T(8,128)S(1)} %fusion.186, bf16[2,5120,1280]{2,1,0:T(8,128)(2,1)} %get-tuple-element.825, bf16[64,1280]{1,0:T(8,128)(2,1)S(1)} %get-tuple-element.801, ...), kind=kOutput, calls=%fused_computation.41.clone.1 | convolution fusion | flops 1685340160 | bytes 28347392 | tf_op jit(solution)/shard_map/while/body/eval_jaxpr/dot_general | solution.py:12
  356.1 13.0 %fusion.187 = bf16[64,1280]{1,0:T(8,128)(2,1)S(1)} fusion(bf16[2,1280,5120]{2,1,0:T(8,128)(2,1)} %get-tuple-element.827, s32[]{:T(128)S(6)} %select_n.310, f32[64,5120]{1,0:T(8,128)S(1)} %fusion.186, bf16[2,5120,1280]{2,1,0:T(8,128)(2,1)} %get-tuple-element.825, bf16[64,1280]{1,0:T(8,128)(2,1)S(1)} %get-tuple-element.801, ...), kind=kOutput, calls=%fused_computation.41.clone.1 | convolution fusion | flops 1685340160 | bytes 28347392 | tf_op jit(solution)/shard_map/while/body/eval_jaxpr/dot_general | solution.py:12
  383.5 13.0 %fusion.187 = bf16[64,1280]{1,0:T(8,128)(2,1)S(1)} fusion(bf16[2,1280,5120]{2,1,0:T(8,128)(2,1)} %get-tuple-element.827, s32[]{:T(128)S(6)} %select_n.310, f32[64,5120]{1,0:T(8,128)S(1)} %fusion.186, bf16[2,5120,1280]{2,1,0:T(8,128)(2,1)} %get-tuple-element.825, bf16[64,1280]{1,0:T(8,128)(2,1)S(1)} %get-tuple-element.801, ...), kind=kOutput, calls=%fused_computation.41.clone.1 | convolution fusion | flops 1685340160 | bytes 28347392 | tf_op jit(solution)/shard_map/while/body/eval_jaxpr/dot_general | solution.py:12
  410.9 13.0 %fusion.187 = bf16[64,1280]{1,0:T(8,128)(2,1)S(1)} fusion(bf16[2,1280,5120]{2,1,0:T(8,128)(2,1)} %get-tuple-element.827, s32[]{:T(128)S(6)} %select_n.310, f32[64,5120]{1,0:T(8,128)S(1)} %fusion.186, bf16[2,5120,1280]{2,1,0:T(8,128)(2,1)} %get-tuple-element.825, bf16[64,1280]{1,0:T(8,128)(2,1)S(1)} %get-tuple-element.801, ...), kind=kOutput, calls=%fused_computation.41.clone.1 | convolution fusion | flops 1685340160 | bytes 28347392 | tf_op jit(solution)/shard_map/while/body/eval_jaxpr/dot_general | solution.py:12
  438.3 13.0 %fusion.187 = bf16[64,1280]{1,0:T(8,128)(2,1)S(1)} fusion(bf16[2,1280,5120]{2,1,0:T(8,128)(2,1)} %get-tuple-element.827, s32[]{:T(128)S(6)} %select_n.310, f32[64,5120]{1,0:T(8,128)S(1)} %fusion.186, bf16[2,5120,1280]{2,1,0:T(8,128)(2,1)} %get-tuple-element.825, bf16[64,1280]{1,0:T(8,128)(2,1)S(1)} %get-tuple-element.801, ...), kind=kOutput, calls=%fused_computation.41.clone.1 | convolution fusion | flops 1685340160 | bytes 28347392 | tf_op jit(solution)/shard_map/while/body/eval_jaxpr/dot_general | solution.py:12
  544.6 19.6 %fusion.161 = (bf16[1,1,1280,5120]{3,2,1,0:T(8,128)(2,1)}, bf16[1,1,1280,5120]{3,2,1,0:T(8,128)(2,1)}) fusion(bf16[2,1,1280,5120]{3,2,1,0:T(8,128)(2,1)} %bitcast.150), kind=kLoop, calls=%fused_computation.152 | loop fusion | bytes 52428800 | tf_op jit(solution)/shard_map/slice | solution.py:101
  564.1 17.8 %fusion.160 = (bf16[1,1,5120,1280]{3,2,1,0:T(8,128)(2,1)}, bf16[1,1,5120,1280]{3,2,1,0:T(8,128)(2,1)}) fusion(bf16[2,1,5120,1280]{3,2,1,0:T(8,128)(2,1)} %bitcast.152), kind=kLoop, calls=%fused_computation.151 | loop fusion | bytes 52428800 | tf_op jit(solution)/shard_map/slice | solution.py:102
  591.6 36.0 %fusion.114 = f32[1280,640]{1,0:T(8,128)} fusion(bf16[2048,1280]{1,0:T(8,128)(2,1)} %all-gather.9.cloned.1.call-done, f32[2048,640]{1,0:T(8,128)} %fusion.118, bf16[2048,1280]{1,0:T(8,128)(2,1)} %all-gather.11.cloned.1.call-done, bf16[1,1,5120,1280]{3,2,1,0:T(8,128)(2,1)} %get-tuple-element.573, s32[]{:T(128)S(6)} %select_n.229), kind=kOutput, calls=%fused_computation.115 | convolution fusion | flops 6739722240 | bytes 20643844 | tf_op jit(solution)/shard_map/dot_general | solution.py:12
  641.1 52.0 %all-gather.7.cloned.1.call-done = bf16[2048,1280]{1,0:T(8,128)(2,1)} async-done(((bf16[256,1280]{1,0:T(8,128)(2,1)}), bf16[2048,1280]{1,0:T(8,128)(2,1)}) %all-gather.7.cloned.1.call-update) | async-done | bytes 5242896 | tf_op jit(solution)/shard_map/all_gather | solution.py:100
  693.0 23.9 %fusion.116 = f32[1280,640]{1,0:T(8,128)} fusion(bf16[2048,1280]{1,0:T(8,128)(2,1)} %all-gather.5.cloned.1.call-done, f32[2048,640]{1,0:T(8,128)} %fusion.122, bf16[2048,1280]{1,0:T(8,128)(2,1)} %all-gather.7.cloned.1.call-done, bf16[1,1,5120,1280]{3,2,1,0:T(8,128)(2,1)} %get-tuple-element.572, s32[]{:T(128)S(6)} %select_n.229), kind=kOutput, calls=%fused_computation.116 | convolution fusion | flops 6739722240 | bytes 20643844 | tf_op jit(solution)/shard_map/dot_general | solution.py:12
  721.4 73.1 %psum.7 = f32[]{:T(128)} all-reduce(f32[]{:T(128)} %get-tuple-element.521), channel_id=1, replica_groups=mesh['stage'=4,'data'=8] {'stage','data'}, use_global_device_ids=true, to_apply=%region_3.4 | all-reduce | flops 1 | bytes 8 | tf_op jit(solution)/shard_map/psum | solution.py:107
  (148 shorter events, 384.9 us)
Async XLA Ops:
  7.2 574.8 %all-gather.9.cloned.1.call-start = ((), (), s32[]{:S(2)}) async-start(), calls=%async_computation.4 | async-start | bytes 5898240 | tf_op jit(solution)/shard_map/all_gather | solution.py:99
  22.0 9.9 %collective-permute-start = (bf16[64,1280]{1,0:T(8,128)(2,1)S(1)}, bf16[64,1280]{1,0:T(8,128)(2,1)S(1)}, u32[]{:S(2)}, u32[]{:S(2)}) collective-permute-start(bf16[64,1280]{1,0:T(8,128)(2,1)S(1)} %get-tuple-element.701), channel_id=1, source_target_pairs={{0,8},{8,16},{16,24},{24,0},{1,9},{9,17},{17,25},{25,1},{2,10},{10... | collective-permute-start | bytes 491528 | tf_op jit(solution)/shard_map/while/body/eval_jaxpr/ppermute | solution.py:74
  45.5 7.2 collective-permute-start
  66.2 7.2 collective-permute-start
  86.9 7.2 collective-permute-start
  107.6 7.2 collective-permute-start
  128.3 7.2 collective-permute-start
  149.0 7.2 collective-permute-start
  169.7 7.2 collective-permute-start
  190.4 7.2 collective-permute-start
  211.2 7.2 collective-permute-start
  231.9 7.2 collective-permute-start
  241.6 350.0 %all-gather.11.cloned.1.call-start = ((), (), s32[]{:S(2)}) async-start(), calls=%async_computation.5 | async-start | bytes 5898240 | tf_op jit(solution)/shard_map/all_gather | solution.py:100
  341.6 7.2 collective-permute-start.1
  369.0 7.2 collective-permute-start.1
  396.5 7.2 collective-permute-start.1
  451.3 7.2 collective-permute-start.1
  478.7 7.2 collective-permute-start.1
  506.1 7.2 collective-permute-start.1
  533.5 7.2 collective-permute-start.1
  543.3 88.2 %all-gather.5.cloned.1.call-start = ((), (), s32[]{:S(2)}) async-start(), calls=%async_computation.2 | async-start | bytes 5898240 | tf_op jit(solution)/shard_map/all_gather | solution.py:99
  544.0 149.0 %all-gather.7.cloned.1.call-start = ((), (), s32[]{:S(2)}) async-start(), calls=%async_computation.3 | async-start | bytes 5898240 | tf_op jit(solution)/shard_map/all_gather | solution.py:100
  627.7 89.2 %all-to-all-start.1 = ((f32[8,160,640]{2,1,0:T(8,128)}), f32[8,160,640]{2,1,0:T(8,128)S(1)}, u32[]{:S(2)}, u32[]{:S(2)}) async-start(f32[8,160,640]{2,1,0:T(8,128)} %bitcast.155), calls=%async_computation.1 | async-start | bytes 6553600 | tf_op jit(solution)/shard_map/all_to_all | solution.py:106
  716.9 103.7 %all-to-all-start = ((f32[8,160,640]{2,1,0:T(8,128)}), f32[8,160,640]{2,1,0:T(8,128)}, u32[]{:S(2)}, u32[]{:S(2)}) async-start(f32[8,160,640]{2,1,0:T(8,128)} %bitcast.154), calls=%async_computation | async-start | bytes 6553600 | tf_op jit(solution)/shard_map/all_to_all | solution.py:106
  (4 other events, 25.0 us)
Sparse Core Ops, SparseCore 0:
  241.7 38.9 all-gather.8
  543.4 42.6 all-gather.10
  588.0 40.6 all-gather.4
  630.5 62.4 all-gather.6

commit v2 on v1

v2 whole, which is shorter than its diff:
```python
import functools

import jax
import jax.numpy as jnp
import numpy as np
from jax import lax
from jax.experimental import pallas as pl
from jax.experimental.pallas import tpu as pltpu
from jax.sharding import PartitionSpec as P

BF = jnp.bfloat16
F32 = jnp.float32
MESH = pl.DeviceIdType.MESH
VMEM_BYTES = 67043328


def gelu_fn(pre_act):
    return jax.nn.gelu(pre_act, approximate=True)


def gelu_and_slope(pre_act):
    c_one, c_two = np.float32(np.sqrt(2.0 / np.pi)), np.float32(0.044715)
    square = pre_act * pre_act
    tanh = jnp.tanh(c_one * (pre_act + c_two * (square * pre_act)))
    cdf = 0.5 * (1.0 + tanh)
    inner = c_one + (c_one * 3 * c_two) * square
    return pre_act * cdf, cdf + (0.5 * pre_act) * ((1.0 - tanh * tanh) * inner)


def matmul(lhs, rhs, dims):
    return lax.dot_general(lhs, rhs, (dims, ((), ())), preferred_element_type=F32)


class Place:
    def __init__(self, n_stage):
        self.stage = lax.axis_index("stage")
        self.data = lax.axis_index("data")
        core = lax.rem(self.data, 2)
        x = lax.rem(lax.div(self.data, 2), 2)
        y = lax.div(self.data, 4)
        self.partner = self.data + 1 - 2 * core
        dx, dy = 2 - 4 * x, 4 - 8 * y
        self.moves = (dx, dy, dx + dy)
        self.next = lax.rem(self.stage + 1, n_stage)
        self.prev = lax.rem(self.stage + n_stage - 1, n_stage)

    def at(self, stage, data):
        return {"stage": stage, "data": data}

    def peers(self):
        yield self.at(self.next, self.data)
        yield self.at(self.prev, self.data)
        yield self.at(self.stage, self.partner)
        for move in self.moves:
            yield self.at(self.stage, self.data + move)

    def barrier(self):
        sem = pltpu.get_barrier_semaphore()
        for peer in self.peers():
            pl.semaphore_signal(sem, inc=1, device_id=peer, device_id_type=MESH)
        pl.semaphore_wait(sem, 6)


def remote(src, dst, send_sem, recv_sem, device):
    return pltpu.make_async_remote_copy(
        src_ref=src, dst_ref=dst, send_sem=send_sem, recv_sem=recv_sem, device_id=device, device_id_type=MESH
    )


class Spread:
    def __init__(self, place, src, dst, n_micro, sems):
        self.place, self.src, self.dst, self.n_micro = place, src, dst, n_micro
        self.own_sem, self.send_sem, self.recv_sem, self.fsend_sem, self.frecv_sem = sems

    def spot(self, slot, data):
        return self.dst.at[lax.div(slot, self.n_micro), data, lax.rem(slot, self.n_micro)]

    def own(self, slot):
        return pltpu.make_async_copy(self.src.at[slot], self.spot(slot, self.place.data), self.own_sem.at[slot])

    def direct(self, slot, k):
        place = self.place
        peer = place.partner if k == 0 else place.data + place.moves[k - 1]
        return remote(
            self.src.at[slot],
            self.spot(slot, place.data),
            self.send_sem.at[slot, k],
            self.recv_sem.at[slot, k],
            place.at(place.stage, peer),
        )

    def relay(self, slot, k):
        place = self.place
        spot = self.spot(slot, place.data + place.moves[k])
        return remote(
            spot, spot, self.fsend_sem.at[slot, k], self.frecv_sem.at[slot, k], place.at(place.stage, place.partner)
        )

    def send(self, slot):
        self.own(slot).start()
        for k in range(4):
            self.direct(slot, k).start()

    def forward(self, slot):
        for k in range(3):
            self.direct(slot, k + 1).wait_recv()
            self.relay(slot, k).start()

    def finish(self, n_slots):
        def body(slot, carry):
            self.own(slot).wait()
            self.direct(slot, 0).wait_recv()
            for k in range(4):
                self.direct(slot, k).wait_send()
            for k in range(3):
                self.relay(slot, k).wait()
            return carry

        lax.fori_loop(0, n_slots, body, 0)


def spread_sems(n_slots):
    dma = pltpu.SemaphoreType.DMA
    return [dma((n_slots,)), dma((n_slots, 4)), dma((n_slots, 4)), dma((n_slots, 3)), dma((n_slots, 3))]


def fwd_kernel(
    n_stage, n_tok, tok_ref, tgt_ref, up_ref, down_ref, hg_ref, slope_ref, top_ref, loss_ref,
    w_up, w_down, h_in, h_out, act, slope, tgt, top, loss,
    up_sem, down_sem, tok_sem, tgt_sem, slope_sem, top_sem, zsend_sem, zrecv_sem, *spread,
):
    n_micro = tok_ref.shape[0]
    n_slots = 2 * n_micro
    d_model, d_ff = w_up.shape[1:]
    up_cols = d_ff // up_sem.shape[1]
    down_cols = d_model // down_sem.shape[1]
    place = Place(n_stage)
    is_first = place.stage == 0
    is_last = place.stage == n_stage - 1

    def load_tok(i):
        return pltpu.make_async_copy(tok_ref.at[i], h_in.at[i], tok_sem.at[i])

    def load_up(v, c):
        cols = pl.ds(c * up_cols, up_cols)
        return pltpu.make_async_copy(up_ref.at[v, 0, :, cols], w_up.at[v, :, cols], up_sem.at[v, c])

    def load_down(v, c):
        cols = pl.ds(c * down_cols, down_cols)
        return pltpu.make_async_copy(down_ref.at[v, 0, :, cols], w_down.at[v, :, cols], down_sem.at[v, c])

    @pl.when(is_first)
    def _():
        for i in range(n_micro):
            load_tok(i).start()

    for v in range(2):
        for c in range(up_sem.shape[1]):
            load_up(v, c).start()
        for c in range(down_sem.shape[1]):
            load_down(v, c).start()
    load_tgt = pltpu.make_async_copy(tgt_ref, tgt, tgt_sem)
    load_tgt.start()
    loss[...] = jnp.zeros_like(loss)
    place.barrier()
    gather = Spread(place, h_in, hg_ref, n_micro, spread)

    def put_slope(slot):
        v, i, b = lax.div(slot, n_micro), lax.rem(slot, n_micro), lax.rem(slot, 2)
        return pltpu.make_async_copy(slope.at[b], slope_ref.at[v, i], slope_sem.at[b])

    def hand_on(slot):
        to = slot + n_micro * lax.div(place.stage, n_stage - 1)
        return remote(
            h_out.at[slot], h_in.at[to], zsend_sem.at[slot], zrecv_sem.at[to], place.at(place.next, place.data)
        )

    def arrive(slot):
        return remote(
            h_out.at[slot], h_in.at[slot], zsend_sem.at[slot], zrecv_sem.at[slot], place.at(place.next, place.data)
        )

    def body(slot, carry):
        v, i, b = lax.div(slot, n_micro), lax.rem(slot, n_micro), lax.rem(slot, 2)
        from_data = jnp.logical_and(is_first, v == 0)
        is_top = jnp.logical_and(is_last, v == 1)

        @pl.when(from_data)
        def _():
            load_tok(i).wait()

        @pl.when(jnp.logical_not(from_data))
        def _():
            arrive(slot).wait_recv()

        gather.send(slot)

        @pl.when(i == 0)
        def _():
            for c in range(up_sem.shape[1]):
                load_up(v, c).wait()

        @pl.when(slot >= 2)
        def _():
            put_slope(slot - 2).wait()

        for c in range(up_sem.shape[1]):
            cols = slice(c * up_cols, (c + 1) * up_cols)
            pre_act = matmul(h_in[slot], w_up[v, :, cols], ((1,), (0,)))
            act_val, slope_val = gelu_and_slope(pre_act)
            act[:, cols] = act_val.astype(BF)
            slope[b, :, cols] = slope_val
        put_slope(slot).start()

        @pl.when(i == 0)
        def _():
            for c in range(down_sem.shape[1]):
                load_down(v, c).wait()

        for c in range(down_sem.shape[1]):
            cols = slice(c * down_cols, (c + 1) * down_cols)
            out_val = matmul(act[...], w_down[v, :, cols], ((1,), (0,)))
            h_out[slot, :, cols] = (h_in[slot, :, cols].astype(F32) + out_val).astype(BF)

        @pl.when(jnp.logical_not(is_top))
        def _():
            hand_on(slot).start()

        @pl.when(is_top)
        def _():
            @pl.when(i == 0)
            def _():
                load_tgt.wait()

            for c in range(d_model // 128):
                cols = slice(c * 128, (c + 1) * 128)
                err = h_out[slot, :, cols].astype(F32) - tgt[i, :, cols].astype(F32)
                loss[...] += err * err
                top[i, :, cols] = (err / n_tok).astype(BF)

        @pl.when(slot >= 2)
        def _():
            gather.forward(slot - 2)

        return carry

    lax.fori_loop(0, n_slots, body, 0)
    loss_ref[...] = loss[...]
    put_top = pltpu.make_async_copy(top, top_ref, top_sem)

    @pl.when(is_last)
    def _():
        put_top.start()

    @pl.when(jnp.logical_not(is_last))
    def _():
        load_tgt.wait()

    gather.forward(n_slots - 2)
    gather.forward(n_slots - 1)
    gather.finish(n_slots)
    put_slope(n_slots - 2).wait()
    put_slope(n_slots - 1).wait()
    n_sent = n_slots - n_micro * lax.div(place.stage, n_stage - 1)

    def drain(slot, carry):
        hand_on(slot).wait_send()
        return carry

    lax.fori_loop(0, n_sent, drain, 0)

    @pl.when(is_last)
    def _():
        put_top.wait()


def forward(n_stage, n_data, tokens, targets, up, down):
    n_micro, seq_len, d_model = tokens.shape
    d_ff = up.shape[3]
    n_slots = 2 * n_micro
    dma = pltpu.SemaphoreType.DMA
    hbm = pl.BlockSpec(memory_space=pl.ANY)
    act_shape = (seq_len, d_model)
    return pl.pallas_call(
        functools.partial(fwd_kernel, n_stage, n_data * n_micro * seq_len),
        out_shape=(
            jax.ShapeDtypeStruct((2, n_data, n_micro, *act_shape), BF),
            jax.ShapeDtypeStruct((2, n_micro, seq_len, d_ff), F32),
            jax.ShapeDtypeStruct((n_micro, *act_shape), BF),
            jax.ShapeDtypeStruct((seq_len, 128), F32),
        ),
        in_specs=[hbm] * 4,
        out_specs=(hbm, hbm, hbm, pl.BlockSpec(memory_space=pltpu.VMEM)),
        scratch_shapes=[
            pltpu.VMEM((2, d_model, d_ff), BF),
            pltpu.VMEM((2, d_ff, d_model), BF),
            pltpu.VMEM((n_slots, *act_shape), BF),
            pltpu.VMEM((n_slots, *act_shape), BF),
            pltpu.VMEM((seq_len, d_ff), BF),
            pltpu.VMEM((2, seq_len, d_ff), F32),
            pltpu.VMEM((n_micro, *act_shape), BF),
            pltpu.VMEM((n_micro, *act_shape), BF),
            pltpu.VMEM((seq_len, 128), F32),
            dma((2, 4)), dma((2, 2)), dma((n_micro,)), dma, dma((2,)), dma, dma((n_slots,)), dma((n_slots,)),
            *spread_sems(n_slots),
        ],
        compiler_params=pltpu.CompilerParams(collective_id=0, has_side_effects=True, vmem_limit_bytes=VMEM_BYTES),
        name="fwd_pipe",
    )(tokens, targets, up, down)


def act_bwd(h_in, grad_out, w_one, w_two):
    act_val, gelu_vjp = jax.vjp(gelu_fn, matmul(h_in, w_one, ((1,), (0,))))
    d_act = matmul(grad_out, w_two, ((1,), (1,))).astype(BF)
    d_pre = gelu_vjp(d_act.astype(F32))[0].astype(BF)
    return act_val.astype(BF), d_pre


def layer_dgrad(slope, grad_out, w_one, w_two):
    d_act = matmul(grad_out, w_two, ((1,), (1,))).astype(BF)
    d_pre = (slope * d_act.astype(F32)).astype(BF)
    return (grad_out.astype(F32) + matmul(d_pre, w_one, ((1,), (1,)))).astype(BF)


def put_slot(buf, val, idx):
    return lax.dynamic_update_slice(buf, val[None], (idx, 0, 0))


def solution(mesh):
    n_stage = mesh.shape["stage"]
    n_data = mesh.shape["data"]

    def device_fn(tokens_loc, targets_loc, up_loc, down_loc):
        n_micro, seq_len, d_model = tokens_loc.shape
        d_ff = up_loc.shape[3]
        n_tok = n_data * n_micro * seq_len
        n_slots = 2 * n_micro
        stage_idx = lax.axis_index("stage")
        data_idx = lax.axis_index("data")
        is_last = stage_idx == n_stage - 1
        bwd_perm = [(src, (src - 1) % n_stage) for src in range(n_stage)]

        h_all, slope, tops, loss = forward(n_stage, n_data, tokens_loc, targets_loc, up_loc, down_loc)
        up_loc = up_loc[:, 0]
        down_loc = down_loc[:, 0]
        slope = slope.reshape(n_slots, seq_len, d_ff)

        def pick(arr, idx):
            return lax.dynamic_index_in_dim(arr, idx, 0, keepdims=False)

        def bwd_slot(tick_idx, state):
            g_in, gstash = state
            slot = tick_idx - (n_stage - 1 - stage_idx)
            valid = (slot >= 0) & (slot < n_slots)
            slot = jnp.clip(slot, 0, n_slots - 1)
            virt = 1 - slot // n_micro
            micro = slot % n_micro
            g_cur = jnp.where(is_last & (virt == 1), pick(tops, micro), g_in)
            pos = virt * n_micro + micro
            gstash = put_slot(gstash, g_cur, jnp.where(valid, pos, n_slots))
            g_out = layer_dgrad(pick(slope, pos), g_cur, pick(up_loc, virt), pick(down_loc, virt))
            return lax.ppermute(g_out, "stage", bwd_perm), gstash

        n_ticks = n_slots + n_stage - 1
        zero_act = jnp.zeros((seq_len, d_model), BF)
        stash0 = jnp.zeros((n_slots + 1, seq_len, d_model), BF)
        _, gstash = lax.fori_loop(0, n_ticks, bwd_slot, (zero_act, stash0))

        f_loc = d_ff // n_data
        ups, downs = [], []
        for virt in range(2):
            h_one = h_all[virt].reshape(-1, d_model)
            g_one = lax.all_gather(gstash[virt * n_micro : (virt + 1) * n_micro].reshape(-1, d_model), "data", tiled=True)
            w_one = lax.dynamic_slice(up_loc[virt], (0, data_idx * f_loc), (d_model, f_loc))
            w_two = lax.dynamic_slice(down_loc[virt], (data_idx * f_loc, 0), (f_loc, d_model))
            act, d_pre = act_bwd(h_one, g_one, w_one, w_two)
            downs.append(matmul(act, g_one, ((0,), (0,))))
            g_up = matmul(h_one, d_pre, ((0,), (0,)))
            ups.append(lax.all_to_all(g_up, "data", 0, 1, tiled=True))
        loss = lax.psum(jnp.sum(loss) / (2.0 * n_tok), ("stage", "data"))
        return loss, jnp.stack(ups)[:, None], jnp.stack(downs)[:, None]

    return jax.shard_map(
        device_fn,
        mesh=mesh,
        in_specs=(P("data"), P("data"), P(None, "stage"), P(None, "stage")),
        out_specs=(P(), P(None, "stage", "data"), P(None, "stage", "data")),
        check_vma=False,
    )
```

time: 851 us -> 643 us (0.76)
  matrix products: 465 us -> 258 us
  waiting for transfers between devices: 114 us -> 26.3 us
  Pallas kernels: 0 us -> 80.6 us
  other arithmetic: 51.9 us -> 19.6 us
  starting transfers between devices: 54.2 us -> 83.2 us
  local copies, waits for them, and re-layouts: 61.8 us -> 81.2 us
    dot_general x39 -> x17, matrix products: 465 us -> 258 us  [matmul(): lax.dot_general(lhs, rhs, (dims, ((), ())), preferred_element_type=F32)]
    pallas_call x0 -> x1, Pallas kernels: none -> 80.6 us  [forward(): pl.pallas_call(functools.partial(fwd_kernel, n_stage, n_data * n_micro *...]
    all_gather x2, waiting for transfers between devices: 52 us -> 0.02 us  [device_fn(): lax.all_gather(gstash[virt * n_micro:(virt + 1) * n_micro].reshape(-1, d_...]
    ppermute x11 -> x0, waiting for transfers between devices: 35.1 us -> none  [fwd_slot(): return (lax.ppermute(h_out, 'stage', fwd_perm), stash, tops, loss)]
    ppermute x11, starting transfers between devices: 42.1 us -> 74.7 us  [bwd_slot(): return (lax.ppermute(g_out, 'stage', bwd_perm), gstash)]
    reduce_sum x11 -> x1, other arithmetic: 17.8 us -> 0.61 us  [device_fn(): loss = lax.psum(jnp.sum(loss) / (2.0 * n_tok), ('stage', 'data'))]
    dot_general x0 -> x2, local copies, waits for them, and re-layouts: none -> 15.9 us  [matmul(): lax.dot_general(lhs, rhs, (dims, ((), ())), preferred_element_type=F32)]
    dynamic_update_slice x22 -> x11, other arithmetic: 25.7 us -> 10.5 us  [put_slot(): return lax.dynamic_update_slice(buf, val[None], (idx, 0, 0))]
  transfers between devices with their start and end apart: 28 -> 15, of which waited for: 23 -> 12; matrix products, arithmetic and copies ran while one was open for 49% -> 24% of each run, Pallas kernels for 0% -> 0%
where the time goes in v2:
time: 643 us; the launch traced here: 636 us
  matrix products  258 us (40%)
  starting transfers between devices  83.2 us (13%)
  local copies, waits for them, and re-layouts  81.2 us (13%)
  Pallas kernels  80.6 us (13%)
  blocking collectives  71.8 us (11%)
  waiting for transfers between devices  26.3 us (4%)
  other arithmetic  19.6 us (3%)
  between operations  15.1 us (2%)
    dot_general x17, matrix products, matmul(): lax.dot_general(lhs, rhs, (dims, ((), ())), preferred_element_type=F32)  258 us
    pallas_call x1, Pallas kernels, forward(): pl.pallas_call(functools.partial(fwd_kernel, n_stage, n_data * n_micro *...  80.6 us
    ppermute x11, starting transfers between devices, bwd_slot(): return (lax.ppermute(g_out, 'stage', bwd_perm), gstash)  74.7 us
    psum x1, blocking collectives, device_fn(): loss = lax.psum(jnp.sum(loss) / (2.0 * n_tok), ('stage', 'data'))  71.8 us
    ppermute x11, waiting for transfers between devices, bwd_slot(): return (lax.ppermute(g_out, 'stage', bwd_perm), gstash)  22.2 us
    slice x1, local copies, waits for them, and re-layouts, device_fn(): up_loc[virt]  19.6 us
    slice x1, local copies, waits for them, and re-layouts, device_fn(): down_loc[virt]  18 us
    dot_general x2, local copies, waits for them, and re-layouts, matmul(): lax.dot_general(lhs, rhs, (dims, ((), ())), preferred_element_type=F32)  15.9 us
  transfers between devices with their start and end apart: 15, of which 12 were waited for; matrix products, arithmetic and copies ran while one was open for 24% of the time, Pallas kernels for 0%

profile of v2, /device:TPU:0, one launch (start us, length us, event | category | flops | bytes accessed | tf_op | source)
XLA Modules:
  0.0 636.2 jit_solution(7382990629618001765)
XLA Ops:
  7.2 80.6 %fwd_pipe.1 = (bf16[2,8,4,64,1280]{4,3,2,1,0:T(8,128)(2,1)}, f32[2,4,64,5120]{3,2,1,0:T(8,128)}, bf16[4,64,1280]{2,1,0:T(8,128)(2,1)}, f32[64,128]{1,0:T(8,128)}) custom-call(bf16[4,64,1280]{2,1,0:T(8,128)(2,1)} %tok_ref.1, bf16[4,64,1280]{2,1,0:T(8,128)(2,1)} %tgt_ref.1, bf16[2,1,1280,5120]{3,2,1,0:T(8,128)(2,1)} %up_ref.1, bf16[2,1,5120,1280]{3,2,1,0:T(8,128)(2,1)} %down_ref.1), custom_call_target="tpu_custom_call" | custom-call | tf_op jit(solution)/shard_map/fwd_pipe/pallas_call | solution.py:284
  88.0 294.9 %while.17 = (s32[]{:T(128)}, bf16[64,1280]{1,0:T(8,128)(2,1)S(1)}, bf16[9,64,1280]{2,1,0:T(8,128)(2,1)S(1)}, s32[]{:T(128)}, pred[]{:T(512)}, /*index=5*/bf16[4,...) while((s32[]{:T(128)}, bf16[64,1280]{1,0:T(8,128)(2,1)S(1)}, ...), condition=%wide.region_3.4_spmd, body=%wide.region_2.3_spmd.sunk | while | flops 1679523840 | bytes 29823040 | solution.py:367
  88.1 17.0 %fusion.131 = bf16[64,1280]{1,0:T(8,128)(2,1)S(1)} fusion(bf16[2,1280,5120]{2,1,0:T(8,128)(2,1)} %get-tuple-element.369, s32[]{:T(128)S(6)} %select_n.152, bf16[2,5120,1280]{2,1,0:T(8,128)(2,1)} %get-tuple-element.368, f32[8,64,5120]{2,1,0:T(8,128)} %get-tuple-element.367, s32[]{:T(128)S(6)} %select_n.154, ...), kind=kOutput, calls=%fused_computation.11.clone.1 | convolution fusion | flops 1679441920 | bytes 28347904 | tf_op jit(solution)/shard_map/while/body/eval_jaxpr/dot_general | solution.py:31
  105.1 31.5 %collective-permute-start = (bf16[64,1280]{1,0:T(8,128)(2,1)S(1)}, bf16[64,1280]{1,0:T(8,128)(2,1)S(1)}, u32[]{:S(2)}, u32[]{:S(2)}) collective-permute-start(bf16[64,1280]{1,0:T(8,128)(2,1)S(1)} %fusion.131), channel_id=1, source_target_pairs={{0,24},{8,0},{16,8},{24,16},{1,25},{9,1},{17,9},{25,17},{2,26},{10... | collective-permute-start | bytes 491528 | tf_op jit(solution)/shard_map/while/body/eval_jaxpr/ppermute | solution.py:362
  141.0 17.0 %fusion.131 = bf16[64,1280]{1,0:T(8,128)(2,1)S(1)} fusion(bf16[2,1280,5120]{2,1,0:T(8,128)(2,1)} %get-tuple-element.369, s32[]{:T(128)S(6)} %select_n.152, bf16[2,5120,1280]{2,1,0:T(8,128)(2,1)} %get-tuple-element.368, f32[8,64,5120]{2,1,0:T(8,128)} %get-tuple-element.367, s32[]{:T(128)S(6)} %select_n.154, ...), kind=kOutput, calls=%fused_computation.11.clone.1 | convolution fusion | flops 1679441920 | bytes 28347904 | tf_op jit(solution)/shard_map/while/body/eval_jaxpr/dot_general | solution.py:31
  165.3 17.0 %fusion.131 = bf16[64,1280]{1,0:T(8,128)(2,1)S(1)} fusion(bf16[2,1280,5120]{2,1,0:T(8,128)(2,1)} %get-tuple-element.369, s32[]{:T(128)S(6)} %select_n.152, bf16[2,5120,1280]{2,1,0:T(8,128)(2,1)} %get-tuple-element.368, f32[8,64,5120]{2,1,0:T(8,128)} %get-tuple-element.367, s32[]{:T(128)S(6)} %select_n.154, ...), kind=kOutput, calls=%fused_computation.11.clone.1 | convolution fusion | flops 1679441920 | bytes 28347904 | tf_op jit(solution)/shard_map/while/body/eval_jaxpr/dot_general | solution.py:31
  189.5 17.0 %fusion.131 = bf16[64,1280]{1,0:T(8,128)(2,1)S(1)} fusion(bf16[2,1280,5120]{2,1,0:T(8,128)(2,1)} %get-tuple-element.369, s32[]{:T(128)S(6)} %select_n.152, bf16[2,5120,1280]{2,1,0:T(8,128)(2,1)} %get-tuple-element.368, f32[8,64,5120]{2,1,0:T(8,128)} %get-tuple-element.367, s32[]{:T(128)S(6)} %select_n.154, ...), kind=kOutput, calls=%fused_computation.11.clone.1 | convolution fusion | flops 1679441920 | bytes 28347904 | tf_op jit(solution)/shard_map/while/body/eval_jaxpr/dot_general | solution.py:31
  213.9 17.0 %fusion.131 = bf16[64,1280]{1,0:T(8,128)(2,1)S(1)} fusion(bf16[2,1280,5120]{2,1,0:T(8,128)(2,1)} %get-tuple-element.369, s32[]{:T(128)S(6)} %select_n.152, bf16[2,5120,1280]{2,1,0:T(8,128)(2,1)} %get-tuple-element.368, f32[8,64,5120]{2,1,0:T(8,128)} %get-tuple-element.367, s32[]{:T(128)S(6)} %select_n.154, ...), kind=kOutput, calls=%fused_computation.11.clone.1 | convolution fusion | flops 1679441920 | bytes 28347904 | tf_op jit(solution)/shard_map/while/body/eval_jaxpr/dot_general | solution.py:31
  238.0 17.0 %fusion.131 = bf16[64,1280]{1,0:T(8,128)(2,1)S(1)} fusion(bf16[2,1280,5120]{2,1,0:T(8,128)(2,1)} %get-tuple-element.369, s32[]{:T(128)S(6)} %select_n.152, bf16[2,5120,1280]{2,1,0:T(8,128)(2,1)} %get-tuple-element.368, f32[8,64,5120]{2,1,0:T(8,128)} %get-tuple-element.367, s32[]{:T(128)S(6)} %select_n.154, ...), kind=kOutput, calls=%fused_computation.11.clone.1 | convolution fusion | flops 1679441920 | bytes 28347904 | tf_op jit(solution)/shard_map/while/body/eval_jaxpr/dot_general | solution.py:31
  262.1 17.1 %fusion.131 = bf16[64,1280]{1,0:T(8,128)(2,1)S(1)} fusion(bf16[2,1280,5120]{2,1,0:T(8,128)(2,1)} %get-tuple-element.369, s32[]{:T(128)S(6)} %select_n.152, bf16[2,5120,1280]{2,1,0:T(8,128)(2,1)} %get-tuple-element.368, f32[8,64,5120]{2,1,0:T(8,128)} %get-tuple-element.367, s32[]{:T(128)S(6)} %select_n.154, ...), kind=kOutput, calls=%fused_computation.11.clone.1 | convolution fusion | flops 1679441920 | bytes 28347904 | tf_op jit(solution)/shard_map/while/body/eval_jaxpr/dot_general | solution.py:31
  286.2 16.9 %fusion.131 = bf16[64,1280]{1,0:T(8,128)(2,1)S(1)} fusion(bf16[2,1280,5120]{2,1,0:T(8,128)(2,1)} %get-tuple-element.369, s32[]{:T(128)S(6)} %select_n.152, bf16[2,5120,1280]{2,1,0:T(8,128)(2,1)} %get-tuple-element.368, f32[8,64,5120]{2,1,0:T(8,128)} %get-tuple-element.367, s32[]{:T(128)S(6)} %select_n.154, ...), kind=kOutput, calls=%fused_computation.11.clone.1 | convolution fusion | flops 1679441920 | bytes 28347904 | tf_op jit(solution)/shard_map/while/body/eval_jaxpr/dot_general | solution.py:31
  310.4 16.9 %fusion.131 = bf16[64,1280]{1,0:T(8,128)(2,1)S(1)} fusion(bf16[2,1280,5120]{2,1,0:T(8,128)(2,1)} %get-tuple-element.369, s32[]{:T(128)S(6)} %select_n.152, bf16[2,5120,1280]{2,1,0:T(8,128)(2,1)} %get-tuple-element.368, f32[8,64,5120]{2,1,0:T(8,128)} %get-tuple-element.367, s32[]{:T(128)S(6)} %select_n.154, ...), kind=kOutput, calls=%fused_computation.11.clone.1 | convolution fusion | flops 1679441920 | bytes 28347904 | tf_op jit(solution)/shard_map/while/body/eval_jaxpr/dot_general | solution.py:31
  334.6 16.9 %fusion.131 = bf16[64,1280]{1,0:T(8,128)(2,1)S(1)} fusion(bf16[2,1280,5120]{2,1,0:T(8,128)(2,1)} %get-tuple-element.369, s32[]{:T(128)S(6)} %select_n.152, bf16[2,5120,1280]{2,1,0:T(8,128)(2,1)} %get-tuple-element.368, f32[8,64,5120]{2,1,0:T(8,128)} %get-tuple-element.367, s32[]{:T(128)S(6)} %select_n.154, ...), kind=kOutput, calls=%fused_computation.11.clone.1 | convolution fusion | flops 1679441920 | bytes 28347904 | tf_op jit(solution)/shard_map/while/body/eval_jaxpr/dot_general | solution.py:31
  358.8 16.9 %fusion.131 = bf16[64,1280]{1,0:T(8,128)(2,1)S(1)} fusion(bf16[2,1280,5120]{2,1,0:T(8,128)(2,1)} %get-tuple-element.369, s32[]{:T(128)S(6)} %select_n.152, bf16[2,5120,1280]{2,1,0:T(8,128)(2,1)} %get-tuple-element.368, f32[8,64,5120]{2,1,0:T(8,128)} %get-tuple-element.367, s32[]{:T(128)S(6)} %select_n.154, ...), kind=kOutput, calls=%fused_computation.11.clone.1 | convolution fusion | flops 1679441920 | bytes 28347904 | tf_op jit(solution)/shard_map/while/body/eval_jaxpr/dot_general | solution.py:31
  384.9 19.6 %fusion.115 = (bf16[1,1,1280,5120]{3,2,1,0:T(8,128)(2,1)}, bf16[1,1,1280,5120]{3,2,1,0:T(8,128)(2,1)}) fusion(bf16[2,1,1280,5120]{3,2,1,0:T(8,128)(2,1)} %bitcast.111), kind=kLoop, calls=%fused_computation.108 | loop fusion | bytes 52428800 | tf_op jit(solution)/shard_map/slice | solution.py:374
  404.5 9.4 %fusion.116 = (bf16[1,8,4,64,1280]{4,3,2,1,0:T(8,128)(2,1)}, bf16[1,8,4,64,1280]{4,3,2,1,0:T(8,128)(2,1)}) fusion(bf16[2,8,4,64,1280]{4,3,2,1,0:T(8,128)(2,1)} %get-tuple-element.234), kind=kLoop, calls=%fused_computation.109 | loop fusion | bytes 20971520 | tf_op jit(solution)/shard_map/slice | solution.py:372
  421.8 9.6 %fusion.72 = f32[2048,640]{1,0:T(8,128)} fusion(bf16[2048,1280]{1,0:T(8,128)(2,1)} %bitcast.117, bf16[1,1,1280,5120]{3,2,1,0:T(8,128)(2,1)} %get-tuple-element.265, s32[]{:T(128)S(6)} %select_n.115), kind=kOutput, calls=%fused_computation.73 | convolution fusion | flops 3355443200 | bytes 12124164 | tf_op jit(solution)/shard_map/dot_general | solution.py:31
  431.4 18.0 %fusion.114 = (bf16[1,1,5120,1280]{3,2,1,0:T(8,128)(2,1)}, bf16[1,1,5120,1280]{3,2,1,0:T(8,128)(2,1)}) fusion(bf16[2,1,5120,1280]{3,2,1,0:T(8,128)(2,1)} %bitcast.113), kind=kLoop, calls=%fused_computation.107 | loop fusion | bytes 52428800 | tf_op jit(solution)/shard_map/slice | solution.py:375
  449.5 17.6 %fusion.48 = f32[8,160,640]{2,1,0:T(8,128)} fusion(bf16[8,160,2048]{2,1,0:T(8,128)(2,1)} %bitcast.119, f32[2048,640]{1,0:T(8,128)} %fusion.72, bf16[2048,1280]{1,0:T(8,128)(2,1)} %all-gather.5.cloned.1.call-done, bf16[1,1,5120,1280]{3,2,1,0:T(8,128)(2,1)} %get-tuple-element.263, s32[]{:T(128)S(6)} %select_n.115), kind=kOutput, calls=%fused_computation.51 | convolution fusion | flops 6739722240 | bytes 20643844 | tf_op jit(solution)/shard_map/dot_general | solution.py:31
  478.8 9.6 %fusion.75 = f32[2048,640]{1,0:T(8,128)} fusion(bf16[2048,1280]{1,0:T(8,128)(2,1)} %bitcast.115, bf16[1,1,1280,5120]{3,2,1,0:T(8,128)(2,1)} %get-tuple-element.264, s32[]{:T(128)S(6)} %select_n.115), kind=kOutput, calls=%fused_computation.76 | convolution fusion | flops 3355443200 | bytes 12124164 | tf_op jit(solution)/shard_map/dot_general | solution.py:31
  488.4 17.9 %fusion.50 = f32[8,160,640]{2,1,0:T(8,128)} fusion(bf16[8,160,2048]{2,1,0:T(8,128)(2,1)} %bitcast.120, f32[2048,640]{1,0:T(8,128)} %fusion.75, bf16[2048,1280]{1,0:T(8,128)(2,1)} %all-gather.3.cloned.1.call-done, bf16[1,1,5120,1280]{3,2,1,0:T(8,128)(2,1)} %get-tuple-element.262, s32[]{:T(128)S(6)} %select_n.115), kind=kOutput, calls=%fused_computation.53 | convolution fusion | flops 6739722240 | bytes 20643844 | tf_op jit(solution)/shard_map/dot_general | solution.py:31
  515.7 71.8 %psum.7 = f32[]{:T(128)} all-reduce(f32[]{:T(128)S(6)} %div.9), channel_id=1, replica_groups=mesh['stage'=4,'data'=8] {'stage','data'}, use_global_device_ids=true, to_apply=%region_1.2 | all-reduce | flops 1 | bytes 8 | tf_op jit(solution)/shard_map/psum | solution.py:380
  587.5 8.1 %convolution_bitcast_fusion = f32[1,640,1280]{2,1,0:T(8,128)S(1)} fusion(bf16[2048,1280]{1,0:T(8,128)(2,1)} %all-gather.5.cloned.1.call-done, f32[2048,640]{1,0:T(8,128)} %fusion.72), kind=kOutput, calls=%fused_computation.47 | convolution fusion | flops 3367239680 | bytes 13762560 | tf_op jit(solution)/shard_map/dot_general | solution.py:31
  595.6 8.1 %convolution_bitcast_fusion.1 = f32[1,640,1280]{2,1,0:T(8,128)S(1)} fusion(bf16[2048,1280]{1,0:T(8,128)(2,1)} %all-gather.3.cloned.1.call-done, f32[2048,640]{1,0:T(8,128)} %fusion.75), kind=kOutput, calls=%fused_computation.48 | convolution fusion | flops 3367239680 | bytes 13762560 | tf_op jit(solution)/shard_map/dot_general | solution.py:31
  (67 shorter events, 131.9 us)
Async XLA Ops:
  7.2 442.3 %all-gather.5.cloned.1.call-start = ((), (), s32[]{:S(2)}) async-start(), calls=%async_computation.3 | async-start | bytes 5898240 | tf_op jit(solution)/shard_map/all_gather | solution.py:373
  105.1 35.9 %collective-permute-start = (bf16[64,1280]{1,0:T(8,128)(2,1)S(1)}, bf16[64,1280]{1,0:T(8,128)(2,1)S(1)}, u32[]{:S(2)}, u32[]{:S(2)}) collective-permute-start(bf16[64,1280]{1,0:T(8,128)(2,1)S(1)} %fusion.131), channel_id=1, source_target_pairs={{0,24},{8,0},{16,8},{24,16},{1,25},{9,1},{17,9},{25,17},{2,26},{10... | collective-permute-start | bytes 491528 | tf_op jit(solution)/shard_map/while/body/eval_jaxpr/ppermute | solution.py:362
  158.0 7.2 %collective-permute-start = (bf16[64,1280]{1,0:T(8,128)(2,1)S(1)}, bf16[64,1280]{1,0:T(8,128)(2,1)S(1)}, u32[]{:S(2)}, u32[]{:S(2)}) collective-permute-start(bf16[64,1280]{1,0:T(8,128)(2,1)S(1)} %fusion.131), channel_id=1, source_target_pairs={{0,24},{8,0},{16,8},{24,16},{1,25},{9,1},{17,9},{25,17},{2,26},{10... | collective-permute-start | bytes 491528 | tf_op jit(solution)/shard_map/while/body/eval_jaxpr/ppermute | solution.py:362
  182.3 7.2 %collective-permute-start = (bf16[64,1280]{1,0:T(8,128)(2,1)S(1)}, bf16[64,1280]{1,0:T(8,128)(2,1)S(1)}, u32[]{:S(2)}, u32[]{:S(2)}) collective-permute-start(bf16[64,1280]{1,0:T(8,128)(2,1)S(1)} %fusion.131), channel_id=1, source_target_pairs={{0,24},{8,0},{16,8},{24,16},{1,25},{9,1},{17,9},{25,17},{2,26},{10... | collective-permute-start | bytes 491528 | tf_op jit(solution)/shard_map/while/body/eval_jaxpr/ppermute | solution.py:362
  206.5 7.2 %collective-permute-start = (bf16[64,1280]{1,0:T(8,128)(2,1)S(1)}, bf16[64,1280]{1,0:T(8,128)(2,1)S(1)}, u32[]{:S(2)}, u32[]{:S(2)}) collective-permute-start(bf16[64,1280]{1,0:T(8,128)(2,1)S(1)} %fusion.131), channel_id=1, source_target_pairs={{0,24},{8,0},{16,8},{24,16},{1,25},{9,1},{17,9},{25,17},{2,26},{10... | collective-permute-start | bytes 491528 | tf_op jit(solution)/shard_map/while/body/eval_jaxpr/ppermute | solution.py:362
  230.9 7.0 %collective-permute-start = (bf16[64,1280]{1,0:T(8,128)(2,1)S(1)}, bf16[64,1280]{1,0:T(8,128)(2,1)S(1)}, u32[]{:S(2)}, u32[]{:S(2)}) collective-permute-start(bf16[64,1280]{1,0:T(8,128)(2,1)S(1)} %fusion.131), channel_id=1, source_target_pairs={{0,24},{8,0},{16,8},{24,16},{1,25},{9,1},{17,9},{25,17},{2,26},{10... | collective-permute-start | bytes 491528 | tf_op jit(solution)/shard_map/while/body/eval_jaxpr/ppermute | solution.py:362
  254.9 7.1 %collective-permute-start = (bf16[64,1280]{1,0:T(8,128)(2,1)S(1)}, bf16[64,1280]{1,0:T(8,128)(2,1)S(1)}, u32[]{:S(2)}, u32[]{:S(2)}) collective-permute-start(bf16[64,1280]{1,0:T(8,128)(2,1)S(1)} %fusion.131), channel_id=1, source_target_pairs={{0,24},{8,0},{16,8},{24,16},{1,25},{9,1},{17,9},{25,17},{2,26},{10... | collective-permute-start | bytes 491528 | tf_op jit(solution)/shard_map/while/body/eval_jaxpr/ppermute | solution.py:362
  279.1 7.0 %collective-permute-start = (bf16[64,1280]{1,0:T(8,128)(2,1)S(1)}, bf16[64,1280]{1,0:T(8,128)(2,1)S(1)}, u32[]{:S(2)}, u32[]{:S(2)}) collective-permute-start(bf16[64,1280]{1,0:T(8,128)(2,1)S(1)} %fusion.131), channel_id=1, source_target_pairs={{0,24},{8,0},{16,8},{24,16},{1,25},{9,1},{17,9},{25,17},{2,26},{10... | collective-permute-start | bytes 491528 | tf_op jit(solution)/shard_map/while/body/eval_jaxpr/ppermute | solution.py:362
  303.1 7.2 %collective-permute-start = (bf16[64,1280]{1,0:T(8,128)(2,1)S(1)}, bf16[64,1280]{1,0:T(8,128)(2,1)S(1)}, u32[]{:S(2)}, u32[]{:S(2)}) collective-permute-start(bf16[64,1280]{1,0:T(8,128)(2,1)S(1)} %fusion.131), channel_id=1, source_target_pairs={{0,24},{8,0},{16,8},{24,16},{1,25},{9,1},{17,9},{25,17},{2,26},{10... | collective-permute-start | bytes 491528 | tf_op jit(solution)/shard_map/while/body/eval_jaxpr/ppermute | solution.py:362
  327.3 7.3 %collective-permute-start = (bf16[64,1280]{1,0:T(8,128)(2,1)S(1)}, bf16[64,1280]{1,0:T(8,128)(2,1)S(1)}, u32[]{:S(2)}, u32[]{:S(2)}) collective-permute-start(bf16[64,1280]{1,0:T(8,128)(2,1)S(1)} %fusion.131), channel_id=1, source_target_pairs={{0,24},{8,0},{16,8},{24,16},{1,25},{9,1},{17,9},{25,17},{2,26},{10... | collective-permute-start | bytes 491528 | tf_op jit(solution)/shard_map/while/body/eval_jaxpr/ppermute | solution.py:362
  351.5 7.2 %collective-permute-start = (bf16[64,1280]{1,0:T(8,128)(2,1)S(1)}, bf16[64,1280]{1,0:T(8,128)(2,1)S(1)}, u32[]{:S(2)}, u32[]{:S(2)}) collective-permute-start(bf16[64,1280]{1,0:T(8,128)(2,1)S(1)} %fusion.131), channel_id=1, source_target_pairs={{0,24},{8,0},{16,8},{24,16},{1,25},{9,1},{17,9},{25,17},{2,26},{10... | collective-permute-start | bytes 491528 | tf_op jit(solution)/shard_map/while/body/eval_jaxpr/ppermute | solution.py:362
  375.7 7.2 %collective-permute-start = (bf16[64,1280]{1,0:T(8,128)(2,1)S(1)}, bf16[64,1280]{1,0:T(8,128)(2,1)S(1)}, u32[]{:S(2)}, u32[]{:S(2)}) collective-permute-start(bf16[64,1280]{1,0:T(8,128)(2,1)S(1)} %fusion.131), channel_id=1, source_target_pairs={{0,24},{8,0},{16,8},{24,16},{1,25},{9,1},{17,9},{25,17},{2,26},{10... | collective-permute-start | bytes 491528 | tf_op jit(solution)/shard_map/while/body/eval_jaxpr/ppermute | solution.py:362
  384.1 104.3 %all-gather.3.cloned.1.call-start = ((), (), s32[]{:S(2)}) async-start(), calls=%async_computation.2 | async-start | bytes 5898240 | tf_op jit(solution)/shard_map/all_gather | solution.py:373
  467.1 42.8 %all-to-all-start.1 = ((f32[8,160,640]{2,1,0:T(8,128)}), f32[8,160,640]{2,1,0:T(8,128)S(1)}, u32[]{:S(2)}, u32[]{:S(2)}) async-start(f32[8,160,640]{2,1,0:T(8,128)} %fusion.48), calls=%async_computation.1 | async-start | bytes 6553600 | tf_op jit(solution)/shard_map/all_to_all | solution.py:379
  506.3 8.1 %copy-start = (f32[64,128]{1,0:T(8,128)S(1)}, f32[64,128]{1,0:T(8,128)}, u32[]{:S(2)}) copy-start(f32[64,128]{1,0:T(8,128)} %get-tuple-element.233) | copy-start | bytes 98308
  509.9 103.7 %all-to-all-start = ((f32[8,160,640]{2,1,0:T(8,128)}), f32[8,160,640]{2,1,0:T(8,128)}, u32[]{:S(2)}, u32[]{:S(2)}) async-start(f32[8,160,640]{2,1,0:T(8,128)} %fusion.50), calls=%async_computation | async-start | bytes 6553600 | tf_op jit(solution)/shard_map/all_to_all | solution.py:379
Sparse Core Ops, SparseCore 0:
  384.2 41.3 all-gather.4
  427.5 40.6 all-gather.2

commit v3 on v2

--- a/solution.py
+++ b/solution.py
@@ -309,6 +309,148 @@
     )(tokens, targets, up, down)
 
 
+def bwd_kernel(
+    n_stage, top_ref, slope_ref, up_ref, down_ref, gg_ref,
+    w_up, w_down, g_in, g_out, d_pre, slope,
+    up_sem, down_sem, top_sem, slope_sem, zsend_sem, zrecv_sem, *spread,
+):
+    n_micro = top_ref.shape[0]
+    n_slots = 2 * n_micro
+    d_model, d_ff = w_up.shape[1:]
+    up_rows = d_model // up_sem.shape[1]
+    down_rows = d_ff // down_sem.shape[1]
+    place = Place(n_stage)
+    is_first = place.stage == 0
+    is_last = place.stage == n_stage - 1
+
+    def load_top(i):
+        return pltpu.make_async_copy(top_ref.at[i], g_in.at[i], top_sem.at[i])
+
+    def load_up(v, c):
+        rows = pl.ds(c * up_rows, up_rows)
+        return pltpu.make_async_copy(up_ref.at[v, 0, rows], w_up.at[v, rows], up_sem.at[v, c])
+
+    def load_down(v, c):
+        rows = pl.ds(c * down_rows, down_rows)
+        return pltpu.make_async_copy(down_ref.at[v, 0, rows], w_down.at[v, rows], down_sem.at[v, c])
+
+    def load_slope(slot):
+        v, i, b = 1 - lax.div(slot, n_micro), lax.rem(slot, n_micro), lax.rem(slot, 2)
+        return pltpu.make_async_copy(slope_ref.at[v, i], slope.at[b], slope_sem.at[b])
+
+    @pl.when(is_last)
+    def _():
+        for i in range(n_micro):
+            load_top(i).start()
+
+    for v in (1, 0):
+        for c in range(down_sem.shape[1]):
+            load_down(v, c).start()
+            if v == 1 and c == 0:
+                load_slope(0).start()
+                load_slope(1).start()
+        for c in range(up_sem.shape[1]):
+            load_up(v, c).start()
+    place.barrier()
+    gather = Spread(place, g_in, gg_ref, n_micro, spread)
+
+    def hand_on(slot):
+        to = slot + n_micro * lax.div(n_stage - 1 - place.stage, n_stage - 1)
+        return remote(
+            g_out.at[slot], g_in.at[to], zsend_sem.at[slot], zrecv_sem.at[to], place.at(place.prev, place.data)
+        )
+
+    def arrive(slot):
+        return remote(
+            g_out.at[slot], g_in.at[slot], zsend_sem.at[slot], zrecv_sem.at[slot], place.at(place.prev, place.data)
+        )
+
+    def body(slot, carry):
+        v, i, b = 1 - lax.div(slot, n_micro), lax.rem(slot, n_micro), lax.rem(slot, 2)
+        from_top = jnp.logical_and(is_last, v == 1)
+        has_next = jnp.logical_not(jnp.logical_and(is_first, v == 0))
+
+        @pl.when(from_top)
+        def _():
+            load_top(i).wait()
+
+        @pl.when(jnp.logical_not(from_top))
+        def _():
+            arrive(slot).wait_recv()
+
+        gather.send(slot)
+
+        @pl.when(i == 0)
+        def _():
+            for c in range(down_sem.shape[1]):
+                load_down(v, c).wait()
+            for c in range(up_sem.shape[1]):
+                load_up(v, c).wait()
+
+        load_slope(slot).wait()
+
+        @pl.when(has_next)
+        def _():
+            for c in range(down_sem.shape[1]):
+                cols = slice(c * down_rows, (c + 1) * down_rows)
+                d_act = matmul(g_in[slot], w_down[v, cols, :], ((1,), (1,))).astype(BF)
+                d_pre[:, cols] = (slope[b, :, cols] * d_act.astype(F32)).astype(BF)
+            for c in range(up_sem.shape[1]):
+                cols = slice(c * up_rows, (c + 1) * up_rows)
+                back = matmul(d_pre[...], w_up[v, cols, :], ((1,), (1,)))
+                g_out[slot, :, cols] = (g_in[slot, :, cols].astype(F32) + back).astype(BF)
+            hand_on(slot).start()
+
+        @pl.when(slot < n_slots - 2)
+        def _():
+            load_slope(slot + 2).start()
+
+        @pl.when(slot >= 2)
+        def _():
+            gather.forward(slot - 2)
+
+        return carry
+
+    lax.fori_loop(0, n_slots, body, 0)
+    gather.forward(n_slots - 2)
+    gather.forward(n_slots - 1)
+    gather.finish(n_slots)
+    n_sent = n_slots - n_micro * lax.div(n_stage - 1 - place.stage, n_stage - 1)
+
+    def drain(slot, carry):
+        hand_on(slot).wait_send()
+        return carry
+
+    lax.fori_loop(0, n_sent, drain, 0)
+
+
+def backward(n_stage, n_data, tops, slope, up, down):
+    n_micro, seq_len, d_model = tops.shape
+    d_ff = up.shape[3]
+    n_slots = 2 * n_micro
+    dma = pltpu.SemaphoreType.DMA
+    hbm = pl.BlockSpec(memory_space=pl.ANY)
+    act_shape = (seq_len, d_model)
+    return pl.pallas_call(
+        functools.partial(bwd_kernel, n_stage),
+        out_shape=jax.ShapeDtypeStruct((2, n_data, n_micro, *act_shape), BF),
+        in_specs=[hbm] * 4,
+        out_specs=hbm,
+        scratch_shapes=[
+            pltpu.VMEM((2, d_model, d_ff), BF),
+            pltpu.VMEM((2, d_ff, d_model), BF),
+            pltpu.VMEM((n_slots, *act_shape), BF),
+            pltpu.VMEM((n_slots, *act_shape), BF),
+            pltpu.VMEM((seq_len, d_ff), BF),
+            pltpu.VMEM((2, seq_len, d_ff), F32),
+            dma((2, 2)), dma((2, 4)), dma((n_micro,)), dma((2,)), dma((n_slots,)), dma((n_slots,)),
+            *spread_sems(n_slots),
+        ],
+        compiler_params=pltpu.CompilerParams(collective_id=1, has_side_effects=True, vmem_limit_bytes=VMEM_BYTES),
+        name="bwd_pipe",
+    )(tops, slope, up, down)
+
+
 def act_bwd(h_in, grad_out, w_one, w_two):
     act_val, gelu_vjp = jax.vjp(gelu_fn, matmul(h_in, w_one, ((1,), (0,))))
     d_act = matmul(grad_out, w_two, ((1,), (1,))).astype(BF)
@@ -316,16 +458,6 @@
     return act_val.astype(BF), d_pre
 
 
-def layer_dgrad(slope, grad_out, w_one, w_two):
-    d_act = matmul(grad_out, w_two, ((1,), (1,))).astype(BF)
-    d_pre = (slope * d_act.astype(F32)).astype(BF)
-    return (grad_out.astype(F32) + matmul(d_pre, w_one, ((1,), (1,)))).astype(BF)
-
-
-def put_slot(buf, val, idx):
-    return lax.dynamic_update_slice(buf, val[None], (idx, 0, 0))
-
-
 def solution(mesh):
     n_stage = mesh.shape["stage"]
     n_data = mesh.shape["data"]
@@ -334,45 +466,16 @@
         n_micro, seq_len, d_model = tokens_loc.shape
         d_ff = up_loc.shape[3]
         n_tok = n_data * n_micro * seq_len
-        n_slots = 2 * n_micro
-        stage_idx = lax.axis_index("stage")
         data_idx = lax.axis_index("data")
-        is_last = stage_idx == n_stage - 1
-        bwd_perm = [(src, (src - 1) % n_stage) for src in range(n_stage)]
-
         h_all, slope, tops, loss = forward(n_stage, n_data, tokens_loc, targets_loc, up_loc, down_loc)
-        up_loc = up_loc[:, 0]
-        down_loc = down_loc[:, 0]
-        slope = slope.reshape(n_slots, seq_len, d_ff)
-
-        def pick(arr, idx):
-            return lax.dynamic_index_in_dim(arr, idx, 0, keepdims=False)
-
-        def bwd_slot(tick_idx, state):
-            g_in, gstash = state
-            slot = tick_idx - (n_stage - 1 - stage_idx)
-            valid = (slot >= 0) & (slot < n_slots)
-            slot = jnp.clip(slot, 0, n_slots - 1)
-            virt = 1 - slot // n_micro
-            micro = slot % n_micro
-            g_cur = jnp.where(is_last & (virt == 1), pick(tops, micro), g_in)
-            pos = virt * n_micro + micro
-            gstash = put_slot(gstash, g_cur, jnp.where(valid, pos, n_slots))
-            g_out = layer_dgrad(pick(slope, pos), g_cur, pick(up_loc, virt), pick(down_loc, virt))
-            return lax.ppermute(g_out, "stage", bwd_perm), gstash
-
-        n_ticks = n_slots + n_stage - 1
-        zero_act = jnp.zeros((seq_len, d_model), BF)
-        stash0 = jnp.zeros((n_slots + 1, seq_len, d_model), BF)
-        _, gstash = lax.fori_loop(0, n_ticks, bwd_slot, (zero_act, stash0))
-
+        g_all = backward(n_stage, n_data, tops, slope, up_loc, down_loc)
         f_loc = d_ff // n_data
         ups, downs = [], []
         for virt in range(2):
             h_one = h_all[virt].reshape(-1, d_model)
-            g_one = lax.all_gather(gstash[virt * n_micro : (virt + 1) * n_micro].reshape(-1, d_model), "data", tiled=True)
-            w_one = lax.dynamic_slice(up_loc[virt], (0, data_idx * f_loc), (d_model, f_loc))
-            w_two = lax.dynamic_slice(down_loc[virt], (data_idx * f_loc, 0), (f_loc, d_model))
+            g_one = g_all[1 - virt].reshape(-1, d_model)
+            w_one = lax.dynamic_slice(up_loc[virt, 0], (0, data_idx * f_loc), (d_model, f_loc))
+            w_two = lax.dynamic_slice(down_loc[virt, 0], (data_idx * f_loc, 0), (f_loc, d_model))
             act, d_pre = act_bwd(h_one, g_one, w_one, w_two)
             downs.append(matmul(act, g_one, ((0,), (0,))))
             g_up = matmul(h_one, d_pre, ((0,), (0,)))

time: 643 us -> 513 us (0.80)
  matrix products: 258 us -> 80.7 us
  Pallas kernels: 80.6 us -> 245 us
  starting transfers between devices: 83.2 us -> 8.12 us
  waiting for transfers between devices: 26.3 us -> 3.82 us
  between operations: 15.1 us -> 1.82 us
  other arithmetic: 19.6 us -> 9.12 us
    dot_general x17 -> x6, matrix products: 258 us -> 80.7 us  [matmul(): lax.dot_general(lhs, rhs, (dims, ((), ())), preferred_element_type=F32)]
    pallas_call x0 -> x1, Pallas kernels: none -> 164 us  [backward(): pl.pallas_call(functools.partial(bwd_kernel, n_stage), out_shape=jax.Shap...]
    ppermute x11 -> x0, starting transfers between devices: 74.7 us -> none  [bwd_slot(): return (lax.ppermute(g_out, 'stage', bwd_perm), gstash)]
    ppermute x11 -> x0, waiting for transfers between devices: 22.2 us -> none  [bwd_slot(): return (lax.ppermute(g_out, 'stage', bwd_perm), gstash)]
    dynamic_update_slice x11 -> x0, other arithmetic: 10.5 us -> none  [put_slot(): return lax.dynamic_update_slice(buf, val[None], (idx, 0, 0))]
  transfers between devices with their start and end apart: 15 -> 2, of which waited for: 12 -> 1; matrix products, arithmetic and copies ran while one was open for 24% -> 12% of each run, Pallas kernels for 0% -> 0%
where the time goes in v3:
time: 513 us; the launch traced here: 503 us
  Pallas kernels  245 us (48%)
  local copies, waits for them, and re-layouts  85.8 us (17%)
  matrix products  80.7 us (16%)
  blocking collectives  69 us (13%)
  other arithmetic  9.12 us (2%)
  starting transfers between devices  8.12 us (2%)
    pallas_call x1, Pallas kernels, backward(): pl.pallas_call(functools.partial(bwd_kernel, n_stage), out_shape=jax.Shap...  164 us
    dot_general x6, matrix products, matmul(): lax.dot_general(lhs, rhs, (dims, ((), ())), preferred_element_type=F32)  80.7 us
    pallas_call x1, Pallas kernels, forward(): pl.pallas_call(functools.partial(fwd_kernel, n_stage, n_data * n_micro *...  80.6 us
    psum x1, blocking collectives, device_fn(): loss = lax.psum(jnp.sum(loss) / (2.0 * n_tok), ('stage', 'data'))  69 us
    slice x1, local copies, waits for them, and re-layouts, device_fn(): up_loc[virt, 0]  20 us
    dot_general x2, local copies, waits for them, and re-layouts, matmul(): lax.dot_general(lhs, rhs, (dims, ((), ())), preferred_element_type=F32)  16 us
  transfers between devices with their start and end apart: 2, of which 1 were waited for; matrix products, arithmetic and copies ran while one was open for 12% of the time, Pallas kernels for 0%

profile of v3, /device:TPU:0, one launch (start us, length us, event | category | flops | bytes accessed | tf_op | source)
XLA Modules:
  0.0 503.4 jit_solution(6775681290462592314)
XLA Ops:
  0.6 20.0 %fusion.87 = (bf16[1,1,1280,5120]{3,2,1,0:T(8,128)(2,1)}, bf16[1,1,1280,5120]{3,2,1,0:T(8,128)(2,1)}) fusion(bf16[2,1,1280,5120]{3,2,1,0:T(8,128)(2,1)} %up_ref.3), kind=kLoop, calls=%fused_computation.93 | loop fusion | bytes 52428800 | tf_op jit(solution)/shard_map/slice | solution.py:477
  20.6 5.4 %copy-done = bf16[2,1,5120,1280]{3,2,1,0:T(8,128)(2,1)S(1)} copy-done((bf16[2,1,5120,1280]{3,2,1,0:T(8,128)(2,1)S(1)}, bf16[2,1,5120,1280]{3,2,1,0:T(8,128)(2,1)}, u32[]{:S(2)}) %copy-start) | copy-done | bytes 26214424
  26.0 8.9 %fusion.86 = (bf16[1,1,5120,1280]{3,2,1,0:T(8,128)(2,1)}, bf16[1,1,5120,1280]{3,2,1,0:T(8,128)(2,1)}) fusion(bf16[2,1,5120,1280]{3,2,1,0:T(8,128)(2,1)S(1)} %copy-done), kind=kLoop, calls=%fused_computation.92 | loop fusion | bytes 52428800 | tf_op jit(solution)/shard_map/slice | solution.py:478
  34.9 80.6 %fwd_pipe.1 = (bf16[2,8,4,64,1280]{4,3,2,1,0:T(8,128)(2,1)}, f32[2,4,64,5120]{3,2,1,0:T(8,128)}, bf16[4,64,1280]{2,1,0:T(8,128)(2,1)}, f32[64,128]{1,0:T(8,128)}) custom-call(bf16[4,64,1280]{2,1,0:T(8,128)(2,1)} %tok_ref.1, bf16[4,64,1280]{2,1,0:T(8,128)(2,1)} %tgt_ref.1, bf16[2,1,1280,5120]{3,2,1,0:T(8,128)(2,1)} %up_ref.3, bf16[2,1,5120,1280]{3,2,1,0:T(8,128)(2,1)} %down_ref.3), custom_call_target="tpu_custom_call" | custom-call | tf_op jit(solution)/shard_map/fwd_pipe/pallas_call | solution.py:284
  115.6 164.3 %bwd_pipe.1 = bf16[2,8,4,64,1280]{4,3,2,1,0:T(8,128)(2,1)} custom-call(bf16[4,64,1280]{2,1,0:T(8,128)(2,1)} %get-tuple-element.9.top_ref, f32[2,4,64,5120]{3,2,1,0:T(8,128)} %get-tuple-element.10.slope_ref, bf16[2,1,1280,5120]{3,2,1,0:T(8,128)(2,1)} %up_ref.3, bf16[2,1,5120,1280]{3,2,1,0:T(8,128)(2,1)} %down_ref.3), custom_call_target="tpu_custom_call" | custom-call | tf_op jit(solution)/shard_map/bwd_pipe/pallas_call | solution.py:434
  279.9 9.2 %fusion.88 = (bf16[1,8,4,64,1280]{4,3,2,1,0:T(8,128)(2,1)}, bf16[1,8,4,64,1280]{4,3,2,1,0:T(8,128)(2,1)}) fusion(bf16[2,8,4,64,1280]{4,3,2,1,0:T(8,128)(2,1)} %bwd_pipe.1), kind=kLoop, calls=%fused_computation.94 | loop fusion | bytes 20971520 | tf_op jit(solution)/shard_map/slice | solution.py:476
  289.2 9.4 %fusion.89 = (bf16[1,8,4,64,1280]{4,3,2,1,0:T(8,128)(2,1)}, bf16[1,8,4,64,1280]{4,3,2,1,0:T(8,128)(2,1)}) fusion(bf16[2,8,4,64,1280]{4,3,2,1,0:T(8,128)(2,1)} %get-tuple-element.8), kind=kLoop, calls=%fused_computation.95 | loop fusion | bytes 20971520 | tf_op jit(solution)/shard_map/slice | solution.py:475
  298.6 8.2 %copy.10 = bf16[1280,2048]{1,0:T(8,128)(2,1)} copy(bf16[1280,2048]{0,1:T(8,128)(2,1)} %bitcast.60) | data formatting | bytes 10485760 | tf_op jit(solution)/shard_map/dot_general | solution.py:31
  306.7 9.6 %fusion.47 = f32[2048,640]{1,0:T(8,128)} fusion(bf16[2048,1280]{1,0:T(8,128)(2,1)} %bitcast.61, bf16[1,1,1280,5120]{3,2,1,0:T(8,128)(2,1)} %get-tuple-element.19, s32[]{:T(128)S(6)} %select_n.2), kind=kOutput, calls=%fused_computation.61 | convolution fusion | flops 3355443200 | bytes 12124164 | tf_op jit(solution)/shard_map/dot_general | solution.py:31
  316.3 27.3 %fusion.22 = f32[8,160,640]{2,1,0:T(8,128)} fusion(bf16[8,160,2048]{2,1,0:T(8,128)(2,1)} %bitcast.67, f32[2048,640]{1,0:T(8,128)} %fusion.47, bf16[2048,1280]{1,0:T(8,128)(2,1)} %bitcast.63, bf16[1,1,5120,1280]{3,2,1,0:T(8,128)(2,1)} %get-tuple-element.17, s32[]{:T(128)S(6)} %select_n.2), kind=kOutput, calls=%fused_computation.38 | convolution fusion | flops 6739722240 | bytes 20643844 | tf_op jit(solution)/shard_map/dot_general | solution.py:31
  343.7 3.7 all-to-all-start
  347.3 7.9 %copy.12 = bf16[1280,2048]{1,0:T(8,128)(2,1)} copy(bf16[1280,2048]{0,1:T(8,128)(2,1)} %bitcast.58) | data formatting | bytes 10485760 | tf_op jit(solution)/shard_map/dot_general | solution.py:31
  355.2 9.5 %fusion.44 = f32[2048,640]{1,0:T(8,128)} fusion(bf16[2048,1280]{1,0:T(8,128)(2,1)} %bitcast.59, bf16[1,1,1280,5120]{3,2,1,0:T(8,128)(2,1)} %get-tuple-element.20, s32[]{:T(128)S(6)} %select_n.2), kind=kOutput, calls=%fused_computation.58 | convolution fusion | flops 3355443200 | bytes 12124164 | tf_op jit(solution)/shard_map/dot_general | solution.py:31
  364.7 18.0 %fusion.20 = f32[8,160,640]{2,1,0:T(8,128)} fusion(bf16[8,160,2048]{2,1,0:T(8,128)(2,1)} %bitcast.68, f32[2048,640]{1,0:T(8,128)} %fusion.44, bf16[2048,1280]{1,0:T(8,128)(2,1)} %bitcast.65, bf16[1,1,5120,1280]{3,2,1,0:T(8,128)(2,1)} %get-tuple-element.18, s32[]{:T(128)S(6)} %select_n.2), kind=kOutput, calls=%fused_computation.36 | convolution fusion | flops 6739722240 | bytes 20643844 | tf_op jit(solution)/shard_map/dot_general | solution.py:31
  382.7 3.8 all-to-all-done
  386.5 4.5 all-to-all-start.1
  392.3 69.0 %psum.7 = f32[]{:T(128)} all-reduce(f32[]{:T(128)S(6)} %div.3), channel_id=1, replica_groups=mesh['stage'=4,'data'=8] {'stage','data'}, use_global_device_ids=true, to_apply=%region_1.0 | all-reduce | flops 1 | bytes 8 | tf_op jit(solution)/shard_map/psum | solution.py:483
  461.3 8.1 %convolution_bitcast_fusion = f32[1,640,1280]{2,1,0:T(8,128)S(1)} fusion(bf16[2048,1280]{1,0:T(8,128)(2,1)} %bitcast.66, f32[2048,640]{1,0:T(8,128)} %fusion.44), kind=kOutput, calls=%fused_computation.32 | convolution fusion | flops 3367239680 | bytes 13762560 | tf_op jit(solution)/shard_map/dot_general | solution.py:31
  469.4 8.1 %convolution_bitcast_fusion.1 = f32[1,640,1280]{2,1,0:T(8,128)S(1)} fusion(bf16[2048,1280]{1,0:T(8,128)(2,1)} %bitcast.64, f32[2048,640]{1,0:T(8,128)} %fusion.47), kind=kOutput, calls=%fused_computation.33 | convolution fusion | flops 3367239680 | bytes 13762560 | tf_op jit(solution)/shard_map/dot_general | solution.py:31
  477.6 3.2 maximum_bitcast_fusion.1
  480.8 3.6 copy.11
  487.6 5.5 %copy.13 = f32[160,8,640]{2,1,0:T(8,128)} copy(f32[160,8,640]{2,0,1:T(8,128)} %bitcast.15) | data formatting | bytes 6553600 | tf_op jit(solution)/shard_map/all_to_all | solution.py:482
  493.1 4.5 stack.19
  497.6 5.3 %maximum_bitcast_fusion = f32[2,1,160,5120]{3,2,1,0:T(8,128)} fusion(f32[1,160,5120]{2,1,0:T(8,128)} %stack.19, f32[1,160,5120]{2,1,0:T(8,128)S(1)} %stack.18), kind=kLoop, calls=%fused_computation.4 | loop fusion | flops 1638400 | bytes 13107200
  (6 shorter events, 3.7 us)
Async XLA Ops:
  0.6 25.4 %copy-start = (bf16[2,1,5120,1280]{3,2,1,0:T(8,128)(2,1)S(1)}, bf16[2,1,5120,1280]{3,2,1,0:T(8,128)(2,1)}, u32[]{:S(2)}) copy-start(bf16[2,1,5120,1280]{3,2,1,0:T(8,128)(2,1)} %down_ref.3) | copy-start | bytes 78643200
  343.7 42.8 %all-to-all-start = ((f32[8,160,640]{2,1,0:T(8,128)}), f32[8,160,640]{2,1,0:T(8,128)S(1)}, u32[]{:S(2)}, u32[]{:S(2)}) async-start(f32[8,160,640]{2,1,0:T(8,128)} %fusion.22), calls=%async_computation | async-start | bytes 6553600 | tf_op jit(solution)/shard_map/all_to_all | solution.py:482
  382.7 8.3 %copy-start.1 = (f32[64,128]{1,0:T(8,128)S(1)}, f32[64,128]{1,0:T(8,128)}, u32[]{:S(2)}) copy-start(f32[64,128]{1,0:T(8,128)} %get-tuple-element.7) | copy-start | bytes 98308
  386.5 101.0 %all-to-all-start.1 = ((f32[8,160,640]{2,1,0:T(8,128)}), f32[8,160,640]{2,1,0:T(8,128)}, u32[]{:S(2)}, u32[]{:S(2)}) async-start(f32[8,160,640]{2,1,0:T(8,128)} %fusion.20), calls=%async_computation.1 | async-start | bytes 6553600 | tf_op jit(solution)/shard_map/all_to_all | solution.py:482

commit v4 on v3

--- a/solution.py
+++ b/solution.py
@@ -451,11 +451,229 @@
     )(tops, slope, up, down)
 
 
-def act_bwd(h_in, grad_out, w_one, w_two):
-    act_val, gelu_vjp = jax.vjp(gelu_fn, matmul(h_in, w_one, ((1,), (0,))))
-    d_act = matmul(grad_out, w_two, ((1,), (1,))).astype(BF)
-    d_pre = gelu_vjp(d_act.astype(F32))[0].astype(BF)
-    return act_val.astype(BF), d_pre
+def wgrad_kernel(
+    n_stage, h_ref, g_ref, up_ref, down_ref, part_ref, gup_ref, gdown_ref, loss_ref,
+    h_buf, g_buf, w_up, w_down, act, d_pre, d_act, acc_down, acc_a, acc_b, parts,
+    h_sem, g_sem, up_sem, down_sem, gd_sem, own_sem, send_sem, recv_sem, csend_sem, crecv_sem, psend_sem, precv_sem,
+):
+    n_data, n_micro, seq_len, d_model = h_ref.shape[1:]
+    f_loc = w_up.shape[3]
+    rows = d_model // n_data
+    n_tok = n_data * seq_len
+    half = d_model // 2
+    wide = acc_b.shape[2]
+    stage, data = lax.axis_index("stage"), lax.axis_index("data")
+    core = lax.rem(data, 2)
+    x = lax.rem(lax.div(data, 2), 2)
+    y = lax.div(data, 4)
+    odd = x + y - 2 * x * y
+    dc, dx, dy = 1 - 2 * core, 2 - 4 * x, 4 - 8 * y
+    other = data + dx * (1 - odd) + dy * odd
+    blocks = (data * (1 - odd) + other * odd, other * (1 - odd) + data * odd)
+    plane = (dc, dx, dx + dc, dy, dy + dc, dx + dy, dx + dy + dc)
+
+    def at(stage_idx, data_idx):
+        return {"stage": stage_idx, "data": data_idx}
+
+    def column(k):
+        return at(lax.rem(stage + k, n_stage), data)
+
+    def block_cols(k):
+        return pl.ds(pl.multiple_of(blocks[k] * f_loc, f_loc), f_loc)
+
+    def load_up(v, k):
+        return pltpu.make_async_copy(up_ref.at[v, 0, :, block_cols(k)], w_up.at[v, k], up_sem.at[v, k])
+
+    def load_down(v, k):
+        return pltpu.make_async_copy(down_ref.at[v, 0, block_cols(k), :], w_down.at[v, k], down_sem.at[v, k])
+
+    def load_h(t):
+        v, i, b = 1 - lax.div(t, n_micro), lax.rem(t, n_micro), lax.rem(t, 2)
+        return pltpu.make_async_copy(h_ref.at[v, :, i], h_buf.at[b], h_sem.at[b])
+
+    def load_g(t):
+        v, i, b = lax.div(t, n_micro), lax.rem(t, n_micro), lax.rem(t, 2)
+        return pltpu.make_async_copy(g_ref.at[v, :, i], g_buf.at[b], g_sem.at[b])
+
+    for v in (1, 0):
+        for k in range(2):
+            load_down(v, k).start()
+            load_up(v, k).start()
+        if v == 1:
+            load_g(0).start()
+            load_h(0).start()
+            load_g(1).start()
+            load_h(1).start()
+
+    sem = pltpu.get_barrier_semaphore()
+    for k in range(1, n_stage):
+        pl.semaphore_signal(sem, inc=1, device_id=column(k), device_id_type=MESH)
+    for move in plane:
+        pl.semaphore_signal(sem, inc=1, device_id=at(stage, data + move), device_id_type=MESH)
+    pl.semaphore_wait(sem, n_stage - 1 + len(plane))
+
+    is_last = stage == n_stage - 1
+
+    def column_send(k):
+        spot = parts.at[data]
+        return remote(spot, spot, csend_sem.at[k - 1], crecv_sem, column(k))
+
+    def plane_send(k):
+        spot = parts.at[data]
+        return remote(spot, spot, psend_sem.at[k], precv_sem.at[k], at(stage, data + plane[k]))
+
+    @pl.when(is_last)
+    def _():
+        total = part_ref[0:8]
+        for k in range(1, seq_len // 8):
+            total = total + part_ref[8 * k : 8 * k + 8]
+        parts[data] = total
+
+    def store_down(v):
+        return pltpu.make_async_copy(acc_down.at[v], gdown_ref.at[v, 0], gd_sem.at[v])
+
+    def pieces(v, kind):
+        for there in range(2):
+            for flip in range(2):
+                to_core = core + flip * dc
+                if kind == 0:
+                    to = data + flip * dc + there * dx
+                    src = acc_a.at[v, pl.ds(pl.multiple_of((to - y * 4) * rows, 8), rows)]
+                else:
+                    to = data + flip * dc + there * dy
+                    first = x * ((2 * rows) % 128) + to_core * rows
+                    src = acc_b.at[v, lax.div(to, 4), pl.ds(pl.multiple_of(first, 8), rows)]
+                yield src, to, 3 * kind + 2 * there + flip - 1
+
+    def exchange(v, kind):
+        for src, to, k in pieces(v, kind):
+            dst = gup_ref.at[v, 0, :, block_cols(kind)]
+            if k == 3 * kind - 1:
+                yield pltpu.make_async_copy(src, dst, own_sem.at[v, kind])
+            else:
+                yield remote(src, dst, send_sem.at[v, k], recv_sem.at[v, k], at(stage, to))
+
+    def body(t, carry):
+        v, i, b = 1 - lax.div(t, n_micro), lax.rem(t, n_micro), lax.rem(t, 2)
+
+        @pl.when(i == 0)
+        def _():
+            for k in range(2):
+                load_down(v, k).wait()
+                load_up(v, k).wait()
+            acc_down[v] = jnp.zeros(acc_down.shape[1:], F32)
+            acc_a[v] = jnp.zeros(acc_a.shape[1:], F32)
+            acc_b[v] = jnp.zeros(acc_b.shape[1:], F32)
+
+        load_g(t).wait()
+        load_h(t).wait()
+        for k in range(2):
+            for r in range(2):
+                part = slice(r * n_data // 2, (r + 1) * n_data // 2)
+                spots = slice(r * n_tok // 2, (r + 1) * n_tok // 2)
+                g_part = g_buf[b, part].reshape(-1, d_model)
+                h_part = h_buf[b, part].reshape(-1, d_model)
+                d_act[spots] = matmul(g_part, w_down[v, k], ((1,), (1,))).astype(BF)
+                act_val, slope_val = gelu_and_slope(matmul(h_part, w_up[v, k], ((1,), (0,))))
+                act[k, spots] = act_val.astype(BF)
+                d_pre[k, spots] = (slope_val * d_act[spots].astype(F32)).astype(BF)
+        a_cols = pl.ds(pl.multiple_of(y * half, half), half)
+        acc_a[v] += matmul(h_buf[b, :, :, a_cols].reshape(n_tok, half), d_pre[0], ((0,), (0,)))
+        for q in range(2):
+            first = q * half + x * (2 * rows - (2 * rows) % 128)
+            b_cols = pl.ds(pl.multiple_of(first, 128), wide)
+            acc_b[v, q] += matmul(h_buf[b, :, :, b_cols].reshape(n_tok, wide), d_pre[1], ((0,), (0,)))
+
+        @pl.when(i == n_micro - 1)
+        def _():
+            for kind in range(2):
+                for copy in exchange(v, kind):
+                    copy.start()
+
+        acc_down[v] += matmul(act[odd], g_buf[b].reshape(n_tok, d_model), ((0,), (0,)))
+
+        @pl.when(i == n_micro - 1)
+        def _():
+            store_down(v).start()
+
+        @pl.when(t < 2 * n_micro - 2)
+        def _():
+            load_g(t + 2).start()
+            load_h(t + 2).start()
+
+        @pl.when(jnp.logical_and(t == 0, is_last))
+        def _():
+            for k in range(1, n_stage):
+                column_send(k).start()
+
+        @pl.when(t == 1)
+        def _():
+            @pl.when(jnp.logical_not(is_last))
+            def _():
+                column_send(1).wait_recv()
+
+            for k in range(len(plane)):
+                plane_send(k).start()
+
+        return carry
+
+    lax.fori_loop(0, 2 * n_micro, body, 0)
+
+    for k in range(len(plane)):
+        plane_send(k).wait()
+    total = parts[0]
+    for k in range(1, n_data):
+        total = total + parts[k]
+    loss_ref[...] = total
+
+    @pl.when(is_last)
+    def _():
+        for k in range(1, n_stage):
+            column_send(k).wait_send()
+
+    for v in (1, 0):
+        store_down(v).wait()
+        for kind in range(2):
+            for copy in exchange(v, kind):
+                copy.wait()
+
+
+def weight_grads(n_stage, n_data, h_all, g_all, up, down, loss):
+    n_micro, seq_len, d_model = h_all.shape[2:]
+    d_ff = up.shape[3]
+    f_loc = d_ff // n_data
+    n_tok = n_data * seq_len
+    wide = -(-(d_model // 4 + (d_model // 4) % 128) // 128) * 128
+    dma = pltpu.SemaphoreType.DMA
+    hbm = pl.BlockSpec(memory_space=pl.ANY)
+    vmem = pl.BlockSpec(memory_space=pltpu.VMEM)
+    return pl.pallas_call(
+        functools.partial(wgrad_kernel, n_stage),
+        out_shape=(
+            jax.ShapeDtypeStruct((2, 1, d_model // n_data, d_ff), F32),
+            jax.ShapeDtypeStruct((2, 1, f_loc, d_model), F32),
+            jax.ShapeDtypeStruct((8, 128), F32),
+        ),
+        in_specs=[hbm] * 4 + [vmem],
+        out_specs=(hbm, hbm, vmem),
+        scratch_shapes=[
+            pltpu.VMEM((2, n_data, seq_len, d_model), BF),
+            pltpu.VMEM((2, n_data, seq_len, d_model), BF),
+            pltpu.VMEM((2, 2, d_model, f_loc), BF),
+            pltpu.VMEM((2, 2, f_loc, d_model), BF),
+            pltpu.VMEM((2, n_tok, f_loc), BF),
+            pltpu.VMEM((2, n_tok, f_loc), BF),
+            pltpu.VMEM((n_tok, f_loc), BF),
+            pltpu.VMEM((2, f_loc, d_model), F32),
+            pltpu.VMEM((2, d_model // 2, f_loc), F32),
+            pltpu.VMEM((2, 2, wide, f_loc), F32),
+            pltpu.VMEM((n_data, 8, 128), F32),
+            dma((2,)), dma((2,)), dma((2, 2)), dma((2, 2)), dma((2,)), dma((2, 2)), dma((2, 6)), dma((2, 6)),
+            dma((n_stage - 1,)), dma, dma((7,)), dma((7,)),
+        ],
+        compiler_params=pltpu.CompilerParams(collective_id=2, has_side_effects=True, vmem_limit_bytes=VMEM_BYTES),
+        name="wgrad",
+    )(h_all, g_all, up, down, loss)
 
 
 def solution(mesh):
@@ -463,25 +681,12 @@
     n_data = mesh.shape["data"]
 
     def device_fn(tokens_loc, targets_loc, up_loc, down_loc):
-        n_micro, seq_len, d_model = tokens_loc.shape
-        d_ff = up_loc.shape[3]
+        n_micro, seq_len, _ = tokens_loc.shape
         n_tok = n_data * n_micro * seq_len
-        data_idx = lax.axis_index("data")
         h_all, slope, tops, loss = forward(n_stage, n_data, tokens_loc, targets_loc, up_loc, down_loc)
         g_all = backward(n_stage, n_data, tops, slope, up_loc, down_loc)
-        f_loc = d_ff // n_data
-        ups, downs = [], []
-        for virt in range(2):
-            h_one = h_all[virt].reshape(-1, d_model)
-            g_one = g_all[1 - virt].reshape(-1, d_model)
-            w_one = lax.dynamic_slice(up_loc[virt, 0], (0, data_idx * f_loc), (d_model, f_loc))
-            w_two = lax.dynamic_slice(down_loc[virt, 0], (data_idx * f_loc, 0), (f_loc, d_model))
-            act, d_pre = act_bwd(h_one, g_one, w_one, w_two)
-            downs.append(matmul(act, g_one, ((0,), (0,))))
-            g_up = matmul(h_one, d_pre, ((0,), (0,)))
-            ups.append(lax.all_to_all(g_up, "data", 0, 1, tiled=True))
-        loss = lax.psum(jnp.sum(loss) / (2.0 * n_tok), ("stage", "data"))
-        return loss, jnp.stack(ups)[:, None], jnp.stack(downs)[:, None]
+        grad_up, grad_down, loss = weight_grads(n_stage, n_data, h_all, g_all, up_loc, down_loc, loss)
+        return jnp.sum(loss) / (2.0 * n_tok), grad_up, grad_down
 
     return jax.shard_map(
         device_fn,

time: 513 us -> 341 us (0.66); the launches traced: 503 us -> 341 us
  Pallas kernels: 245 us -> 328 us
  matrix products: 80.7 us -> 0 us
  local copies, waits for them, and re-layouts: 85.8 us -> 9.36 us
  blocking collectives: 69 us -> 0 us
  starting transfers between devices: 8.12 us -> 0 us
  other arithmetic: 9.12 us -> 1.44 us
    pallas_call x0 -> x1, Pallas kernels: none -> 82.7 us  [weight_grads(): pl.pallas_call(functools.partial(wgrad_kernel, n_stage), out_shape=(jax.S...]
    dot_general x6 -> x0, matrix products: 80.7 us -> none  [matmul(): lax.dot_general(lhs, rhs, (dims, ((), ())), preferred_element_type=F32)]
    psum x1 -> x0, blocking collectives: 69 us -> none  [device_fn(): loss = lax.psum(jnp.sum(loss) / (2.0 * n_tok), ('stage', 'data'))]
    slice x4 -> x0, local copies, waits for them, and re-layouts: 47.5 us -> none  [the longest x1 20 us: device_fn(): up_loc[virt, 0]]
    dot_general x2 -> x0, local copies, waits for them, and re-layouts: 16 us -> none  [matmul(): lax.dot_general(lhs, rhs, (dims, ((), ())), preferred_element_type=F32)]
    all_to_all x2 -> x0, local copies, waits for them, and re-layouts: 9.15 us -> none  [device_fn(): ups.append(lax.all_to_all(g_up, 'data', 0, 1, tiled=True))]
    unnamed x2 -> x1, other arithmetic: 8.51 us -> 0.01 us
    all_to_all x2 -> x0, starting transfers between devices: 8.12 us -> none  [device_fn(): ups.append(lax.all_to_all(g_up, 'data', 0, 1, tiled=True))]
  transfers between devices with their start and end apart: 2 -> 0, of which waited for: 1 -> 0; matrix products, arithmetic and copies ran while one was open for 12% -> 0% of each run, Pallas kernels for 0% -> 0%
where the time goes in v4:
time: 341 us
  Pallas kernels  328 us (96%)
  local copies, waits for them, and re-layouts  9.36 us (3%)
    pallas_call x1, Pallas kernels, backward(): pl.pallas_call(functools.partial(bwd_kernel, n_stage), out_shape=jax.Shap...  164 us
    pallas_call x1, Pallas kernels, weight_grads(): pl.pallas_call(functools.partial(wgrad_kernel, n_stage), out_shape=(jax.S...  82.7 us
    pallas_call x1, Pallas kernels, forward(): pl.pallas_call(functools.partial(fwd_kernel, n_stage, n_data * n_micro *...  80.6 us
    unnamed x6, local copies, waits for them, and re-layouts  9.36 us

profile of v4, /device:TPU:0, one launch (start us, length us, event | category | flops | bytes accessed | tf_op | source)
XLA Modules:
  0.0 340.9 jit_solution(9319819383810020904)
XLA Ops:
  0.6 80.6 %fwd_pipe.1 = (bf16[2,8,4,64,1280]{4,3,2,1,0:T(8,128)(2,1)}, f32[2,4,64,5120]{3,2,1,0:T(8,128)}, bf16[4,64,1280]{2,1,0:T(8,128)(2,1)}, f32[64,128]{1,0:T(8,128)}) custom-call(bf16[4,64,1280]{2,1,0:T(8,128)(2,1)} %tok_ref.1, bf16[4,64,1280]{2,1,0:T(8,128)(2,1)} %tgt_ref.1, bf16[2,1,1280,5120]{3,2,1,0:T(8,128)(2,1)} %up_ref.5, bf16[2,1,5120,1280]{3,2,1,0:T(8,128)(2,1)} %down_ref.5), custom_call_target="tpu_custom_call" | custom-call | tf_op jit(solution)/shard_map/fwd_pipe/pallas_call | solution.py:284
  81.3 164.4 %bwd_pipe.1.g_ref = bf16[2,8,4,64,1280]{4,3,2,1,0:T(8,128)(2,1)} custom-call(bf16[4,64,1280]{2,1,0:T(8,128)(2,1)} %get-tuple-element.11.top_ref, f32[2,4,64,5120]{3,2,1,0:T(8,128)} %get-tuple-element.12.slope_ref, bf16[2,1,1280,5120]{3,2,1,0:T(8,128)(2,1)} %up_ref.5, bf16[2,1,5120,1280]{3,2,1,0:T(8,128)(2,1)} %down_ref.5), custom_call_target="tpu_custom_call" | custom-call | tf_op jit(solution)/shard_map/bwd_pipe/pallas_call | solution.py:434
  245.6 82.7 %wgrad.1 = (f32[2,1,160,5120]{3,2,1,0:T(8,128)}, f32[2,1,640,1280]{3,2,1,0:T(8,128)}, f32[8,128]{1,0:T(8,128)}) custom-call(bf16[2,8,4,64,1280]{4,3,2,1,0:T(8,128)(2,1)} %get-tuple-element.10.h_ref, bf16[2,8,4,64,1280]{4,3,2,1,0:T(8,128)(2,1)} %bwd_pipe.1.g_ref, bf16[2,1,1280,5120]{3,2,1,0:T(8,128)(2,1)} %up_ref.5, bf16[2,1,5120,1280]{3,2,1,0:T(8,128)(2,1)} %down_ref.5, ...), custom_call_target="tpu_custom_call" | custom-call | tf_op jit(solution)/shard_map/wgrad/pallas_call | solution.py:650
  328.3 0.0 slice-start
  328.3 1.4 reduce_sum.9
  330.4 0.0 slice-start.1
  330.4 6.6 %copy.9 = f32[2,1,160,5120]{3,2,1,0:T(8,128)} copy(f32[2,1,160,5120]{3,2,1,0:T(8,128)} %get-tuple-element.21) | data formatting | bytes 13107200
  337.0 0.0 slice-done
  337.0 0.0 slice-done.1
  337.0 2.8 copy.10
  (1 shorter events, 0.0 us)
Async XLA Ops:
  328.3 8.7 %slice-start = ((s8[6553600]{0:T(1024)(128)(4,1)}), s8[2359296]{0:T(1024)(128)(4,1)S(1)}, s32[]{:S(2)}) async-start(s8[6553600]{0:T(1024)(128)(4,1)} %bitcast), calls=%async_computation | async-start | bytes 4718592
  330.4 6.6 %slice-start.1 = ((s8[6553600]{0:T(1024)(128)(4,1)}), s8[4194304]{0:T(1024)(128)(4,1)S(1)}, s32[]{:S(2)}) async-start(s8[6553600]{0:T(1024)(128)(4,1)} %bitcast), calls=%async_computation.1 | async-start | bytes 8388608

commit v5 on v1

v5 whole, which is shorter than its diff:
```python
import functools

import jax
import jax.numpy as jnp
import numpy as np
from jax import lax
from jax.experimental import pallas as pl
from jax.experimental.pallas import tpu as pltpu
from jax.sharding import PartitionSpec as P

BF = jnp.bfloat16
F32 = jnp.float32
MESH = pl.DeviceIdType.MESH
VMEM_BYTES = 67043328
NN, NT, TN = ((1,), (0,)), ((1,), (1,)), ((0,), (0,))


def matmul(lhs, rhs, dims):
    return lax.dot_general(lhs, rhs, (dims, ((), ())), preferred_element_type=F32)


def gelu_and_slope(pre_act):
    c_one, c_two = np.float32(np.sqrt(2.0 / np.pi)), np.float32(0.044715)
    square = pre_act * pre_act
    tanh = jnp.tanh(c_one * (pre_act + c_two * (square * pre_act)))
    cdf = 0.5 * (1.0 + tanh)
    inner = c_one + (c_one * 3 * c_two) * square
    return pre_act * cdf, cdf + (0.5 * pre_act) * ((1.0 - tanh * tanh) * inner)


def local(src, dst, sem):
    return pltpu.make_async_copy(src, dst, sem)


def remote(src, dst, send_sem, recv_sem, device):
    return pltpu.make_async_remote_copy(
        src_ref=src, dst_ref=dst, send_sem=send_sem, recv_sem=recv_sem, device_id=device, device_id_type=MESH
    )


def ds(start, size):
    return pl.ds(start if isinstance(start, int) else pl.multiple_of(start, size), size)


def when(*terms):
    cond = terms[0]
    for term in terms[1:]:
        cond = jnp.logical_and(cond, term)
    return pl.when(cond)


class Place:
    def __init__(self, n_stage):
        self.n_stage = n_stage
        self.stage = stage = lax.axis_index("stage")
        self.data = data = lax.axis_index("data")
        self.core = lax.rem(data, 2)
        self.x = lax.rem(lax.div(data, 2), 2)
        self.y = lax.div(data, 4)
        self.dc, self.dx, self.dy = 1 - 2 * self.core, 2 - 4 * self.x, 4 - 8 * self.y
        self.odd = self.x + self.y - 2 * self.x * self.y
        self.first = lax.div(n_stage - 1 - stage, n_stage - 1)
        self.last = lax.div(stage, n_stage - 1)
        self.is_first = stage == 0
        self.is_last = stage == n_stage - 1
        self.plane = (self.dc, self.dx, self.dx + self.dc, self.dy, self.dy + self.dc)
        self.plane += (self.dx + self.dy, self.dx + self.dy + self.dc)

    def peer(self, move):
        return {"stage": self.stage, "data": self.data + move}

    def column(self, k):
        return {"stage": lax.rem(self.stage + k, self.n_stage), "data": self.data}

    def barrier(self):
        sem = pltpu.get_barrier_semaphore()
        peers = [self.column(k) for k in range(1, self.n_stage)] + [self.peer(move) for move in self.plane]
        for peer in peers:
            pl.semaphore_signal(sem, inc=1, device_id=peer, device_id_type=MESH)
        pl.semaphore_wait(sem, len(peers))


class Spread:
    def __init__(self, place, src, dst, n_micro, sems):
        self.place, self.src, self.dst, self.n_micro = place, src, dst, n_micro
        self.moves = (place.dx, place.dy, place.dx + place.dy)
        self.own_sem, self.send_sem, self.recv_sem, self.fsend_sem, self.frecv_sem = sems

    def spot(self, slot, data):
        rows = ds(data * self.src.shape[1], self.src.shape[1])
        return self.dst.at[lax.div(slot, self.n_micro), lax.rem(slot, self.n_micro), rows]

    def own(self, slot):
        return local(self.src.at[slot], self.spot(slot, self.place.data), self.own_sem.at[slot])

    def direct(self, slot, k):
        move = self.place.dc if k == 0 else self.moves[k - 1]
        spot = self.spot(slot, self.place.data)
        return remote(
            self.src.at[slot], spot, self.send_sem.at[slot, k], self.recv_sem.at[slot, k], self.place.peer(move)
        )

    def relay(self, slot, k):
        spot = self.spot(slot, self.place.data + self.moves[k])
        return remote(
            spot, spot, self.fsend_sem.at[slot, k], self.frecv_sem.at[slot, k], self.place.peer(self.place.dc)
        )

    def send(self, slot):
        self.own(slot).start()
        for k in range(4):
            self.direct(slot, k).start()

    def forward(self, slot):
        for k in range(3):
            self.direct(slot, k + 1).wait_recv()
            self.relay(slot, k).start()

    def sent(self, slot):
        self.own(slot).wait()
        for k in range(4):
            self.direct(slot, k).wait_send()

    def ready(self, slot):
        self.direct(slot, 0).wait_recv()
        for k in range(3):
            self.relay(slot, k).wait_recv()

    def drain(self, n_slots):
        def body(slot, carry):
            for k in range(3):
                self.relay(slot, k).wait_send()
            return carry

        lax.fori_loop(0, n_slots, body, 0)


def kernel(
    n_stage, pieces, tok_ref, tgt_ref, up_ref, down_ref, gup_ref, gdown_ref, loss_ref, hg_ref, gg_ref, slope_ref,
    w_up, w_down, held, out, mid, slope, sq_err, parts, acc_down, acc_a, acc_b,
    up_sem, down_sem, tok_sem, tgt_sem, slope_sem, fsend_sem, frecv_sem, bsend_sem, brecv_sem,
    wu_sem, wd_sem, hbuf_sem, gbuf_sem, gd_sem, own_sem, xsend_sem, xrecv_sem, csend_sem, crecv_sem, psend_sem, precv_sem,
    *spread,
):
    n_micro, seq_len, d_model = tok_ref.shape
    n_data = hg_ref.shape[2] // seq_len
    n_slots = 2 * n_micro
    d_ff = up_ref.shape[3]
    f_loc = d_ff // n_data
    rows = d_model // n_data
    half = d_model // 2
    wide = acc_b.shape[1]
    n_chunk = n_data * seq_len
    n_tok = n_micro * n_chunk
    n_up, n_down = up_sem.shape[1], down_sem.shape[1]
    up_cols, down_cols = d_ff // n_up, d_model // n_down
    place = Place(n_stage)
    first, is_first, is_last, odd = place.first, place.is_first, place.is_last, place.odd


    def load_tok(i):
        return local(tok_ref.at[i], held.at[i], tok_sem.at[i])

    def load_up(v, c):
        cols = pl.ds(c * up_cols, up_cols)
        return local(up_ref.at[v, 0, :, cols], w_up.at[v, :, cols], up_sem.at[v, c])

    def load_down(v, c):
        cols = pl.ds(c * down_cols, down_cols)
        return local(down_ref.at[v, 0, :, cols], w_down.at[v, :, cols], down_sem.at[v, c])

    def load_tgt(i):
        return local(tgt_ref.at[i], held.at[i], tgt_sem)

    @when(is_first)
    def _():
        for i in range(n_micro):
            load_tok(i).start()

    for v in range(2):
        for c in range(n_up):
            load_up(v, c).start()
        for c in range(n_down):
            load_down(v, c).start()

    sq_err[...] = jnp.zeros_like(sq_err)
    place.barrier()
    gather_h = Spread(place, held, hg_ref, n_micro, spread[:5])
    gather_g = Spread(place, held, gg_ref, n_micro, spread[5:])

    def put_slope(slot):
        v, i, b = lax.div(slot, n_micro), lax.rem(slot, n_micro), lax.rem(slot, 2)
        return local(slope.at[b], slope_ref.at[v, i], slope_sem.at[b])

    def fwd_piece(slot, cols):
        to = slot + n_micro * place.last
        src = out.at[lax.rem(slot, 2), :, cols]
        return remote(src, held.at[to, :, cols], fsend_sem.at[slot], frecv_sem.at[to], place.column(1))

    def fwd_whole(slot):
        src = out.at[lax.rem(slot, 2)]
        return remote(src, held.at[slot], fsend_sem.at[slot], frecv_sem.at[slot], place.column(1))

    def fwd_slot(slot, carry):
        v, i, b = lax.div(slot, n_micro), lax.rem(slot, n_micro), lax.rem(slot, 2)
        from_data = jnp.logical_and(is_first, v == 0)
        is_top = jnp.logical_and(is_last, v == 1)

        @when(from_data)
        def _():
            load_tok(i).wait()

        @when(jnp.logical_not(from_data))
        def _():
            fwd_whole(slot).wait_recv()

        gather_h.send(slot)

        @when(v == 1)
        def _():
            gather_h.sent(slot - n_micro)

            @when(is_last)
            def _():
                load_tgt(i).start()

        @when(i == 0)
        def _():
            for c in range(n_up):
                load_up(v, c).wait()

        @when(slot >= 2)
        def _():
            put_slope(slot - 2).wait()

        for c in range(n_up):
            cols = slice(c * up_cols, (c + 1) * up_cols)
            act_val, slope_val = gelu_and_slope(matmul(held[slot], w_up[v, :, cols], NN))
            mid[:, cols] = act_val.astype(BF)
            slope[b, :, cols] = slope_val
        put_slope(slot).start()

        @when(i == 0)
        def _():
            for c in range(n_down):
                load_down(v, c).wait()

        @when(slot >= 2, jnp.logical_not(jnp.logical_and(is_last, slot >= n_micro + 2)))
        def _():
            fwd_whole(slot - 2).wait_send()

        for start, size in pieces:
            cols = slice(start, start + size)
            out_val = matmul(mid[...], w_down[v, :, cols], NN)
            out[b, :, cols] = (held[slot, :, cols].astype(F32) + out_val).astype(BF)

            @when(jnp.logical_not(is_top))
            def _():
                fwd_piece(slot, pl.ds(start, size)).start()

        @when(is_top)
        def _():
            load_tgt(i).wait()
            for c in range(d_model // 128):
                cols = slice(c * 128, (c + 1) * 128)
                err = out[b, :, cols].astype(F32) - held[i, :, cols].astype(F32)
                sq_err[...] += err * err
                held[i, :, cols] = (err / n_tok).astype(BF)

        @when(slot >= 2)
        def _():
            gather_h.forward(slot - 2)

        return carry

    lax.fori_loop(0, n_slots, fwd_slot, 0)

    def column_send(k):
        spot = parts.at[place.data]
        return remote(spot, spot, csend_sem.at[k - 1], crecv_sem, place.column(k))

    def plane_send(k):
        spot = parts.at[place.data]
        return remote(spot, spot, psend_sem.at[k], precv_sem.at[k], place.peer(place.plane[k]))

    @when(is_last)
    def _():
        total = sq_err[0:8]
        for k in range(1, seq_len // 8):
            total = total + sq_err[8 * k : 8 * k + 8]
        parts[place.data] = total


    def load_slope(slot):
        v, i, b = 1 - lax.div(slot, n_micro), lax.rem(slot, n_micro), lax.rem(slot, 2)
        return local(slope_ref.at[v, i], slope.at[b], slope_sem.at[b])

    for slot in range(2):
        put_slope(n_slots - 2 + slot).wait()
        load_slope(slot).start()

    def bwd_piece(slot, cols):
        to = slot + n_micro * first
        src = out.at[lax.rem(slot, 2), :, cols]
        return remote(src, held.at[to, :, cols], bsend_sem.at[slot], brecv_sem.at[to], place.column(n_stage - 1))

    def bwd_whole(slot):
        src = out.at[lax.rem(slot, 2)]
        return remote(src, held.at[slot], bsend_sem.at[slot], brecv_sem.at[slot], place.column(n_stage - 1))

    def bwd_slot(slot):
        p, i, b = lax.div(slot, n_micro), lax.rem(slot, n_micro), lax.rem(slot, 2)
        v = 1 - p

        @when(jnp.logical_not(jnp.logical_and(is_last, p == 0)))
        def _():
            bwd_whole(slot).wait_recv()

        gather_g.send(slot)

        @when(jnp.logical_not(jnp.logical_and(is_first, p == 1)))
        def _():
            load_slope(slot).wait()
            for c in range(n_up):
                cols = slice(c * up_cols, (c + 1) * up_cols)
                d_act = matmul(held[slot], w_down[v, cols, :], NT).astype(BF)
                mid[:, cols] = (slope[b, :, cols] * d_act.astype(F32)).astype(BF)

            @when(p == 0)
            def _():
                gather_h.sent(slot + n_micro)

            @when(slot >= 2)
            def _():
                bwd_whole(slot - 2).wait_send()

            @when(slot < 2, jnp.logical_not(is_last))
            def _():
                fwd_whole(n_slots - 2 + slot).wait_send()

            for start, size in pieces:
                cols = slice(start, start + size)
                back = matmul(mid[...], w_up[v, cols, :], NT)
                out[b, :, cols] = (held[slot, :, cols].astype(F32) + back).astype(BF)
                bwd_piece(slot, pl.ds(start, size)).start()

            @when(i < n_micro - 2)
            def _():
                load_slope(slot + 2).start()


    other = place.data + place.dx * (1 - odd) + place.dy * odd
    blocks = (place.data * (1 - odd) + other * odd, other * (1 - odd) + place.data * odd)

    def wd_rows(p, k):
        return pl.ds(pl.multiple_of(p * (2 * f_loc + 4 * n_chunk) + k * f_loc, 128), f_loc)

    def wu_cols(p, k):
        return pl.ds(pl.multiple_of((5 * p + k) * f_loc, 128), f_loc)

    def buf_rows(n, k):
        return pl.ds(pl.multiple_of(2 * f_loc + (2 * k + lax.rem(n, 2)) * n_chunk, 128), n_chunk)

    def act_cols(k):
        return pl.ds(pl.multiple_of((2 + k) * f_loc, 128), f_loc)

    def block_cols(k):
        return ds(blocks[k] * f_loc, f_loc)

    def load_wu(p, k):
        return local(up_ref.at[1 - p, 0, :, block_cols(k)], w_up.at[1, :, wu_cols(p, k)], wu_sem.at[p, k])

    def load_wd(p, k):
        return local(down_ref.at[1 - p, 0, block_cols(k), :], w_down.at[1, wd_rows(p, k), :], wd_sem.at[p, k])

    def load_h(n):
        p, c, b = lax.div(n, n_micro), lax.rem(n, n_micro), lax.rem(n, 2)
        return local(hg_ref.at[1 - p, c], w_down.at[1, buf_rows(n, 0), :], hbuf_sem.at[b])

    def load_g(n):
        p, c, b = lax.div(n, n_micro), lax.rem(n, n_micro), lax.rem(n, 2)
        return local(gg_ref.at[p, c], w_down.at[1, buf_rows(n, 1), :], gbuf_sem.at[b])

    def h_ready(n):
        p, c = lax.div(n, n_micro), lax.rem(n, n_micro)
        gather_h.ready((1 - p) * n_micro + c)

    def store_down(v):
        return local(acc_down, gdown_ref.at[v, 0], gd_sem)

    def exchange(v, kind):
        for there in range(2):
            for flip in range(2):
                k = 3 * kind + 2 * there + flip - 1
                move = flip * place.dc + there * (place.dx if kind == 0 else place.dy)
                to = place.data + move
                if kind == 0:
                    src = acc_a.at[pl.ds(pl.multiple_of((to - place.y * 4) * rows, 8), rows)]
                else:
                    start = place.x * ((2 * rows) % 128) + lax.rem(to, 2) * rows
                    src = acc_b.at[lax.div(to, 4), pl.ds(pl.multiple_of(start, 8), rows)]
                dst = gup_ref.at[v, 0, :, block_cols(kind)]
                if there == flip == 0:
                    yield functools.partial(local, src, dst, own_sem.at[v, kind])
                else:
                    yield functools.partial(remote, src, dst, xsend_sem.at[v, k], xrecv_sem.at[v, k], place.peer(move))

    def wait_sent(v):
        for kind in range(2):
            for k, copy in enumerate(exchange(v, kind)):
                if k == 0:
                    copy().wait()
                else:
                    copy().wait_send()
        store_down(v).wait()

    def chunk(n):
        p, c = lax.div(n, n_micro), lax.rem(n, n_micro)
        v = 1 - p
        h_rows, g_rows = buf_rows(n, 0), buf_rows(n, 1)
        gather_g.own(n).wait()
        gather_g.ready(n)
        load_g(n).start()

        @when(n < n_slots - 1)
        def _():
            h_ready(n + 1)
            load_h(n + 1).start()

        @when(c == 0)
        def _():
            for k in range(2):
                load_wu(p, k).wait()
                load_wd(p, k).wait()

            @when(p == 1)
            def _():
                wait_sent(1)

            acc_down[...] = jnp.zeros(acc_down.shape, F32)
            acc_a[...] = jnp.zeros(acc_a.shape, F32)
            acc_b[...] = jnp.zeros(acc_b.shape, F32)

        load_h(n).wait()
        part = n_chunk // 2
        for k in range(2):
            for r in range(2):
                spots = pl.ds(r * part, part)
                h_part = w_down[1, pl.ds(pl.multiple_of(h_rows.start + r * part, 64), part), :]
                act_val, slope_val = gelu_and_slope(matmul(h_part, w_up[1, :, wu_cols(p, k)], NN))
                w_up[1, spots, act_cols(k)] = act_val.astype(BF)
                for j in range(n_data // 2):
                    cols = slice((r * n_data // 2 + j) * f_loc, (r * n_data // 2 + j + 1) * f_loc)
                    slope[k, :, cols] = slope_val[j * seq_len : (j + 1) * seq_len]
        load_g(n).wait()
        for k in range(2):
            for r in range(2):
                g_part = w_down[1, pl.ds(pl.multiple_of(g_rows.start + r * part, 64), part), :]
                d_act = matmul(g_part, w_down[1, wd_rows(p, k), :], NT).astype(BF).astype(F32)
                for j in range(n_data // 2):
                    cols = slice((r * n_data // 2 + j) * f_loc, (r * n_data // 2 + j + 1) * f_loc)
                    d_pre = slope[k, :, cols] * d_act[j * seq_len : (j + 1) * seq_len]
                    spots = pl.ds(n_chunk + r * part + j * seq_len, seq_len)
                    w_up[1, spots, act_cols(k)] = d_pre.astype(BF)

        def d_pre_of(k):
            return w_up[1, pl.ds(n_chunk, n_chunk), act_cols(k)]

        acc_a[...] += matmul(w_down[1, h_rows, ds(place.y * half, half)], d_pre_of(0), TN)
        for q in range(2):
            start = q * half + place.x * (2 * rows - (2 * rows) % 128)
            b_cols = pl.ds(pl.multiple_of(start, 128), wide)
            acc_b[q] += matmul(w_down[1, h_rows, b_cols], d_pre_of(1), TN)

        @when(c == n_micro - 1)
        def _():
            for kind in range(2):
                for copy in exchange(v, kind):
                    copy().start()

        act_own = w_up[1, pl.ds(0, n_chunk), pl.ds(pl.multiple_of((2 + odd) * f_loc, 128), f_loc)]
        acc_down[...] += matmul(act_own, w_down[1, g_rows, :], TN)

        @when(c == n_micro - 1)
        def _():
            store_down(v).start()

    n_steps = 2 * n_micro

    def bwd_step(t, carry):
        p, u = lax.div(t, n_steps), lax.rem(t, n_steps)

        @when(u < n_micro)
        def _():
            bwd_slot(p * n_micro + u)

        @when(t == n_micro - 1)
        def _():
            for q in range(2):
                for k in range(2):
                    load_wu(q, k).start()
                    load_wd(q, k).start()
            h_ready(0)
            load_h(0).start()

        c = u - n_micro + 2 * p * first

        @when(c >= 0, c < n_micro)
        def _():
            chunk(p * n_micro + c)

        f = u - 2 + p * first

        @when(f >= 0, f < n_micro)
        def _():
            gather_g.forward(p * n_micro + f)

        @when(t < 2)
        def _():
            gather_h.forward(n_slots - 2 + t)

        @when(t == n_steps - 1, jnp.logical_not(is_first))
        def _():
            for slot in range(n_micro, n_micro + 2):
                load_slope(slot).start()

        @when(t == 0, is_last)
        def _():
            for k in range(1, n_stage):
                column_send(k).start()

        @when(t == 1)
        def _():
            @when(jnp.logical_not(is_last))
            def _():
                column_send(1).wait_recv()

            for k in range(len(place.plane)):
                plane_send(k).start()

        return carry

    lax.fori_loop(0, 2 * n_steps, bwd_step, 0)


    for k in range(len(place.plane)):
        plane_send(k).wait()
    total = parts[0]
    for k in range(1, n_data):
        total = total + parts[k]
    loss_ref[0, 0] = jnp.sum(total) / (2.0 * n_tok)

    @when(is_last)
    def _():
        for k in range(1, n_stage):
            column_send(k).wait_send()

    def drain_z(i, carry):
        bwd_whole(i + n_slots - 2 - n_micro * first).wait_send()
        return carry

    lax.fori_loop(0, 2, drain_z, 0)
    gather_h.drain(n_slots)
    gather_g.drain(n_slots)

    def drain_g(slot, carry):
        for k in range(4):
            gather_g.direct(slot, k).wait_send()
        return carry

    lax.fori_loop(0, n_slots, drain_g, 0)
    wait_sent(0)
    for v in range(2):
        for kind in range(2):
            for k, copy in enumerate(exchange(v, kind)):
                if k > 0:
                    copy().wait_recv()


def solution(mesh):
    n_stage = mesh.shape["stage"]
    n_data = mesh.shape["data"]

    def device_fn(tokens, targets, up, down):
        n_micro, seq_len, d_model = tokens.shape
        d_ff = up.shape[3]
        f_loc = d_ff // n_data
        n_slots = 2 * n_micro
        wide = -(-(d_model // 4 + (d_model // 4) % 128) // 128) * 128
        sizes = (d_model // 5, 2 * d_model // 5, 2 * d_model // 5) if d_model % 640 == 0 else (d_model // 2,) * 2
        pieces = tuple((sum(sizes[:k]), size) for k, size in enumerate(sizes))
        dma = pltpu.SemaphoreType.DMA
        hbm = pl.BlockSpec(memory_space=pl.ANY)
        vmem = pltpu.VMEM
        act_shape = (seq_len, d_model)
        gathered = jax.ShapeDtypeStruct((2, n_micro, n_data * seq_len, d_model), BF)
        spread = [dma((n_slots,)), dma((n_slots, 4)), dma((n_slots, 4)), dma((n_slots, 3)), dma((n_slots, 3))]
        grad_up, grad_down, loss, *_ = pl.pallas_call(
            functools.partial(kernel, n_stage, pieces),
            out_shape=(
                jax.ShapeDtypeStruct((2, 1, d_model // n_data, d_ff), F32),
                jax.ShapeDtypeStruct((2, 1, f_loc, d_model), F32),
                jax.ShapeDtypeStruct((1, 1), F32),
                gathered,
                gathered,
                jax.ShapeDtypeStruct((2, n_micro, seq_len, d_ff), F32),
            ),
            in_specs=[hbm] * 4,
            out_specs=(hbm, hbm, pl.BlockSpec(memory_space=pltpu.SMEM), hbm, hbm, hbm),
            scratch_shapes=[
                vmem((2, d_model, d_ff), BF),
                vmem((2, d_ff, d_model), BF),
                vmem((n_slots, *act_shape), BF),
                vmem((2, *act_shape), BF),
                vmem((seq_len, d_ff), BF),
                vmem((2, seq_len, d_ff), F32),
                vmem((seq_len, 128), F32),
                vmem((n_data, 8, 128), F32),
                vmem((f_loc, d_model), F32),
                vmem((d_model // 2, f_loc), F32),
                vmem((2, wide, f_loc), F32),
                dma((2, 4)), dma((2, 2)), dma((n_micro,)), dma, dma((2,)),
                dma((n_slots,)), dma((n_slots,)), dma((n_slots,)), dma((n_slots,)),
                dma((2, 2)), dma((2, 2)), dma((2,)), dma((2,)), dma, dma((2, 2)), dma((2, 6)), dma((2, 6)),
                dma((n_stage - 1,)), dma, dma((7,)), dma((7,)),
                *spread, *spread,
            ],
            compiler_params=pltpu.CompilerParams(collective_id=0, has_side_effects=True, vmem_limit_bytes=VMEM_BYTES),
            name="step",
        )(tokens, targets, up, down)
        return loss.reshape(()), grad_up, grad_down

    return jax.shard_map(
        device_fn,
        mesh=mesh,
        in_specs=(P("data"), P("data"), P(None, "stage"), P(None, "stage")),
        out_specs=(P(), P(None, "stage", "data"), P(None, "stage", "data")),
        check_vma=False,
    )
```

time: 851 us -> 312 us (0.37)
  matrix products: 465 us -> 0 us
  Pallas kernels: 0 us -> 300 us
  waiting for transfers between devices: 114 us -> 0 us
  blocking collectives: 73.1 us -> 0 us
  starting transfers between devices: 54.2 us -> 0 us
  local copies, waits for them, and re-layouts: 61.8 us -> 9.36 us
  other arithmetic: 51.9 us -> 0.01 us
  between operations: 14.1 us -> 2.62 us
  loops' own time: 8.67 us -> 0 us
    dot_general x39 -> x0, matrix products: 465 us -> none  [matmul(): lax.dot_general(lhs, rhs, (dims, ((), ())), preferred_element_type=jnp.fl...]
    pallas_call x0 -> x1, Pallas kernels: none -> 300 us  [device_fn(): pl.pallas_call(functools.partial(kernel, n_stage, pieces), out_shape=(jax...]
    psum x1 -> x0, blocking collectives: 73.1 us -> none  [device_fn(): loss = lax.psum(loss, ('stage', 'data'))]
    ppermute x22 -> x0, waiting for transfers between devices: 60.5 us -> none  [the longest x11 35.1 us: fwd_slot(): return (lax.ppermute(h_out, 'stage', fwd_perm), stash, tops, loss)]
    all_gather x4 -> x0, waiting for transfers between devices: 52 us -> none  [the longest x2 52 us: device_fn(): lax.all_gather(gstash[virt * n_micro:(virt + 1) * n_micro].reshape(-1, d_...]
    ppermute x22 -> x0, starting transfers between devices: 45.8 us -> none  [the longest x11 42.1 us: bwd_slot(): return (lax.ppermute(g_out, 'stage', bwd_perm), gstash)]
    slice x4 -> x0, local copies, waits for them, and re-layouts: 42.3 us -> none  [the longest x1 19.6 us: device_fn(): up_loc[virt]]
    dynamic_update_slice x22 -> x0, other arithmetic: 25.7 us -> none  [put_slot(): return lax.dynamic_update_slice(buf, val[None], (idx, 0, 0))]
  transfers between devices with their start and end apart: 28 -> 0, of which waited for: 23 -> 0; matrix products, arithmetic and copies ran while one was open for 49% -> 0% of each run, Pallas kernels for 0% -> 0%
where the time goes in v5:
time: 312 us
  Pallas kernels  300 us (96%)
  local copies, waits for them, and re-layouts  9.36 us (3%)
    pallas_call x1, Pallas kernels, device_fn(): pl.pallas_call(functools.partial(kernel, n_stage, pieces), out_shape=(jax...  300 us
    unnamed x6, local copies, waits for them, and re-layouts  9.36 us

profile of v5, /device:TPU:0, one launch (start us, length us, event | category | flops | bytes accessed | tf_op | source)
XLA Modules:
  0.0 311.7 jit_solution(11606290203863823851)
XLA Ops:
  0.6 299.7 %step.1 = (f32[2,1,160,5120]{3,2,1,0:T(8,128)}, f32[2,1,640,1280]{3,2,1,0:T(8,128)}, f32[1,1]{1,0:T(1,128)}, bf16[2,4,512,1280]{3,2,1,0:T(8,128)(2,1)}, bf16[2,4...) custom-call(bf16[4,64,1280]{2,1,0:T(8,128)(2,1)} %tok_ref.1, bf16[4,64,1280]{2,1,0:T(8,128)(2,1)} %tgt_ref.1, ...), custom_call_target="tpu_custom_call" | custom-call | tf_op jit(solution)/shard_map/step/pallas_call | solution.py:598
  300.4 0.0 slice-start
  301.2 0.0 slice-start.1
  301.2 6.6 %copy.11 = f32[2,1,160,5120]{3,2,1,0:T(8,128)} copy(f32[2,1,160,5120]{3,2,1,0:T(8,128)} %get-tuple-element.13) | data formatting | bytes 13107200
  307.8 0.0 slice-done
  307.8 0.0 slice-done.1
  307.8 2.8 copy.12
  (1 shorter events, 0.0 us)
Async XLA Ops:
  300.4 7.4 %slice-start = ((s8[6553600]{0:T(1024)(128)(4,1)}), s8[2359296]{0:T(1024)(128)(4,1)S(1)}, s32[]{:S(2)}) async-start(s8[6553600]{0:T(1024)(128)(4,1)} %bitcast.1), calls=%async_computation | async-start | bytes 4718592
  301.2 6.6 %slice-start.1 = ((s8[6553600]{0:T(1024)(128)(4,1)}), s8[4194304]{0:T(1024)(128)(4,1)S(1)}, s32[]{:S(2)}) async-start(s8[6553600]{0:T(1024)(128)(4,1)} %bitcast.1), calls=%async_computation.1 | async-start | bytes 8388608
